TPU v7x, 512 devices: a whole 4x4x16 slice. The times are simulated.
512 devices in a mesh: gx: 16 (over y, z_hi, core), gy: 32 (over z_lo, x).
Axes of the slice: x: 4, y: 4, z: 16 (z_hi: 2, z_lo: 8; z = z_hi * 8 + z_lo), core: 2. Of those that a mesh axis runs over, the one named last changes fastest.
Arguments:
- permeability: float32 [3, 8, 128, 4096], P(None, None, 'gx', 'gy'), may hold values from 0.01 to 10
- layer_map: int32 [8], replicated, may hold values from 0 to 3, never falling along the last dimension, each value on 1 to 3 neighbouring positions
Outputs:
- coarse_perm: float32 [3, 4, 16, 512], P(None, None, 'gx', 'gy')
- coarse_trans: float32 [3, 4, 16, 512], P(None, None, 'gx', 'gy')
Inputs may be any that keep to these rules, and one draw needn't show every extreme that they name: layer_map never falls along the fine layers and every one of the 4 coarse layers holds one or more fine layers.
All inputs are finite; a program needn't handle non-finite values.
Results may differ from a plain program's by a relative error of at most 0.0003.
Values sent between devices are 32-bit elements; how exact they have to be, the bound alone decides.
A program may use at most 64 MiB of HBM per device.

v0:
```python
import math

import jax
import jax.numpy as jnp
from jax import lax
from jax.sharding import PartitionSpec as P

NCL = 4
BXY = 8
SWEEPS = 4


KMIN = 0.01
EPS = 1e-06


def with_halo(block, sides, width):
    for axis, dim in sides:
        count = lax.axis_size(axis)
        forward = [(i, i + 1) for i in range(count - 1)]
        backward = [(target, source) for source, target in forward]
        low = lax.ppermute(
            lax.slice_in_dim(block, block.shape[dim] - width, None, axis=dim), axis, forward
        )
        high = lax.ppermute(lax.slice_in_dim(block, 0, width, axis=dim), axis, backward)
        block = jnp.concatenate([low, block, high], axis=dim)
    return block


def shifted(value, axis, steps):
    count = lax.axis_size(axis)
    initial, last = (max(0, -steps), min(count, count - steps))
    return lax.ppermute(value, axis, [(source, source + steps) for source in range(initial, last)])


def sweep_weights(count):
    return [
        1.0 / (1.05 + 0.95 * math.cos(math.pi * (2 * s + 1) / (2 * count))) for s in range(count)
    ]


def harmonic(left, right):
    return 2.0 * left * right / (left + right)


def linear_field(depth, width, height):
    zc = (jnp.arange(depth + 2, dtype=jnp.float32) - 0.5 - depth / 2.0) / depth
    xc = (jnp.arange(width + 2, dtype=jnp.float32) - 0.5 - width / 2.0) / width
    yc = (jnp.arange(height + 2, dtype=jnp.float32) - 0.5 - height / 2.0) / height
    shape = (depth + 2, width + 2, height + 2)
    return jnp.stack(
        [
            jnp.broadcast_to(xc[None, :, None], shape),
            jnp.broadcast_to(yc[None, None, :], shape),
            jnp.broadcast_to(zc[:, None, None], shape),
        ]
    )


def patch_partials(kext, layer_map):
    depth, width, height = (kext.shape[1], kext.shape[2], kext.shape[3])
    perm = kext + KMIN
    tx = jnp.concatenate(
        [perm[0][:, :1], harmonic(perm[0][:, :-1], perm[0][:, 1:]), perm[0][:, -1:]], axis=1
    )
    ty = jnp.concatenate(
        [perm[1][:, :, :1], harmonic(perm[1][:, :, :-1], perm[1][:, :, 1:]), perm[1][:, :, -1:]],
        axis=2,
    )
    tz = jnp.concatenate([perm[2][:1], harmonic(perm[2][:-1], perm[2][1:]), perm[2][-1:]], axis=0)
    diag = tx[:, :-1] + tx[:, 1:] + ty[:, :, :-1] + ty[:, :, 1:] + tz[:-1] + tz[1:]
    inverse = 1.0 / diag
    ghost = linear_field(depth, width, height)

    def inflow_of(full):
        inflow = tx[:, 1:] * full[:, 1:-1, 2:, 1:-1] + tx[:, :-1] * full[:, 1:-1, :-2, 1:-1]
        inflow = (
            inflow
            + ty[:, :, 1:] * full[:, 1:-1, 1:-1, 2:]
            + ty[:, :, :-1] * full[:, 1:-1, 1:-1, :-2]
        )
        return inflow + tz[1:] * full[:, 2:, 1:-1, 1:-1] + tz[:-1] * full[:, :-2, 1:-1, 1:-1]

    boundary = inflow_of(ghost.at[:, 1:-1, 1:-1, 1:-1].set(0.0))
    pressure = ghost[:, 1:-1, 1:-1, 1:-1]
    for weight in sweep_weights(SWEEPS):
        padded = jnp.pad(pressure, ((0, 0), (1, 1), (1, 1), (1, 1)))
        change = inflow_of(padded) + boundary - diag * pressure
        pressure = pressure + weight * (change * inverse)
    full = ghost.at[:, 1:-1, 1:-1, 1:-1].set(pressure)
    drop = jnp.stack(
        [
            full[0, 1:-1, 1:-1, 1:-1] - full[0, 1:-1, 2:, 1:-1],
            full[1, 1:-1, 1:-1, 1:-1] - full[1, 1:-1, 1:-1, 2:],
            full[2, 1:-1, 1:-1, 1:-1] - full[2, 2:, 1:-1, 1:-1],
        ]
    )
    faces = jnp.stack([tx[:, 1:], ty[:, :, 1:], tz[1:]])
    square = drop * drop
    energy = faces * square
    onehot = (layer_map[:, None] == jnp.arange(NCL, dtype=jnp.int32)[None, :]).astype(jnp.float32)

    def coarsen(values):
        blocks = values.reshape(3, depth, width // BXY, BXY, height // BXY, BXY).sum(axis=(3, 5))
        return jnp.einsum("dzab,zl->dlab", blocks, onehot, precision=lax.Precision.HIGHEST)

    return (coarsen(energy), coarsen(square))


def fold_owned(padded):
    rows = padded[:, :, :, 2:-2]
    rows = rows.at[:, :, :, 0].add(padded[:, :, :, 0])
    rows = rows.at[:, :, :, -1].add(padded[:, :, :, -1])
    owned = rows[:, :, :, :, 2:-2]
    owned = owned.at[:, :, :, :, 0].add(rows[:, :, :, :, 0])
    owned = owned.at[:, :, :, :, -1].add(rows[:, :, :, :, -1])
    return owned


def local(permeability, layer_map):
    kext = with_halo(permeability, (("gx", 2), ("gy", 3)), BXY)
    energy, square = patch_partials(kext, layer_map)
    stacked = jnp.stack([energy, square])
    gathered = with_halo(stacked, (("gx", 3), ("gy", 4)), 1)
    owned = fold_owned(gathered)
    coarse_perm = owned[0] / (owned[1] + EPS)
    upper_x = shifted(coarse_perm[0], "gx", -1)
    upper_y = shifted(coarse_perm[1][:, :, :1], "gy", -1)
    trans_x = harmonic(coarse_perm[0], jnp.concatenate([coarse_perm[0][:, 1:], upper_x], axis=1))
    trans_y = harmonic(coarse_perm[1], jnp.concatenate([coarse_perm[1][:, :, 1:], upper_y], axis=2))
    trans_z = jnp.concatenate(
        [harmonic(coarse_perm[2][:-1], coarse_perm[2][1:]), jnp.zeros_like(coarse_perm[2][:1])],
        axis=0,
    )
    return (coarse_perm, jnp.stack([trans_x, trans_y, trans_z]))


def solution(mesh):
    in_specs = (P(None, None, "gx", "gy"), P())
    out_specs = (P(None, None, "gx", "gy"), P(None, None, "gx", "gy"))
    return jax.shard_map(local, mesh=mesh, in_specs=in_specs, out_specs=out_specs, check_vma=False)
```

profile of v0, /device:TPU:57, one launch (start us, length us, event | category | flops | bytes accessed | tf_op | source)
XLA Modules:
  0.0 160.8 jit_solution(1488632224507451930)
XLA Ops:
  0.6 15.1 %collective-permute-start = (f32[3,8,8,128]{3,2,1,0:T(8,128)}, f32[3,8,8,128]{3,2,1,0:T(8,128)S(1)}, u32[]{:S(2)}, u32[]{:S(2)}) collective-permute-start(f32[3,8,8,128]{3,2,1,0:T(8,128)} %param.14), channel_id=1, source_target_pairs={{0,32},{32,64},{64,96},{96,128},{128,160},{160,192},{192,224},{224... | collective-permute-start | bytes 294920 | tf_op jit(solution)/shard_map/ppermute | solution.py:22
  15.7 1.9 %collective-permute-start.1 = (f32[3,8,8,128]{3,2,1,0:T(8,128)}, f32[3,8,8,128]{3,2,1,0:T(8,128)S(1)}, u32[]{:S(2)}, u32[]{:S(2)}) collective-permute-start(f32[3,8,8,128]{3,2,1,0:T(8,128)} %param.14), channel_id=1, source_target_pairs={{32,0},{64,32},{96,64},{128,96},{160,128},{192,160},{224,192},{256... | collective-permute-start | bytes 294920 | tf_op jit(solution)/shard_map/ppermute | solution.py:25
  18.6 13.9 %collective-permute-done.1 = f32[3,8,8,128]{3,2,1,0:T(8,128)S(1)} collective-permute-done((f32[3,8,8,128]{3,2,1,0:T(8,128)}, f32[3,8,8,128]{3,2,1,0:T(8,128)S(1)}, u32[]{:S(2)}, u32[]{:S(2)}) %collective-permute-start.1) | collective-permute-done | bytes 98336 | tf_op jit(solution)/shard_map/ppermute | solution.py:25
  33.4 2.2 %collective-permute-start.2 = (f32[3,8,24,8]{3,2,1,0:T(8,128)}, f32[3,8,24,8]{3,2,1,0:T(8,128)}, u32[]{:S(2)}, u32[]{:S(2)}) collective-permute-start(f32[3,8,24,8]{3,2,1,0:T(8,128)} %get-tuple-element.100), channel_id=1, source_target_pairs={{0,1},{1,2},{2,3},{3,4},{4,5},{5,6},{6,7},{7,8},{8,9},{9,10},{10,1... | collective-permute-start | bytes 55304 | tf_op jit(solution)/shard_map/ppermute | solution.py:22
  35.7 5.4 %collective-permute-start.3 = (f32[3,8,24,8]{3,2,1,0:T(8,128)}, f32[3,8,24,8]{3,2,1,0:T(8,128)}, u32[]{:S(2)}, u32[]{:S(2)}) collective-permute-start(f32[3,8,24,8]{3,2,1,0:T(8,128)} %get-tuple-element.101), channel_id=1, source_target_pairs={{1,0},{2,1},{3,2},{4,3},{5,4},{6,5},{7,6},{8,7},{9,8},{10,9},{11,1... | collective-permute-start | bytes 55304 | tf_op jit(solution)/shard_map/ppermute | solution.py:25
  41.7 13.7 %scatter.6 = f32[3,10,26,146]{3,2,1,0:T(8,128)S(1)} dynamic-update-slice(f32[3,10,26,146]{3,2,1,0:T(8,128)S(1)} %pad_maximum_fusion, f32[3,8,24,144]{3,2,1,0:T(8,128)S(1)} %broadcast.243, s32[]{:T(128)} %constant.191.clone.1, s32[]{:T(128)} %constant.192.clone.1, s32[]{:T(128)} %constant.192.clone.1, s32[]{:T(128)} %constant.192.clone.1) | dynamic-update-slice | bytes 663556 | tf_op jit(solution)/shard_map/scatter | solution.py:84
  63.7 2.0 %stack.44 = f32[1,8,3,8,18,8]{5,4,3,2,1,0:T(8,128)} reshape(f32[8,24,144]{2,1,0:T(8,128)S(1)} %get-tuple-element.87) | data formatting | bytes 221184 | tf_op jit(solution)/shard_map/stack | solution.py:98
  65.7 2.0 %stack.45 = f32[1,8,3,8,18,8]{5,4,3,2,1,0:T(8,128)} reshape(f32[8,24,144]{2,1,0:T(8,128)S(1)} %get-tuple-element.88) | data formatting | bytes 221184 | tf_op jit(solution)/shard_map/stack | solution.py:98
  72.0 13.7 %scatter.9 = f32[3,10,26,146]{3,2,1,0:T(8,128)S(1)} dynamic-update-slice(f32[3,10,26,146]{3,2,1,0:T(8,128)S(1)} %copy.34, f32[3,8,24,144]{3,2,1,0:T(8,128)S(1)} %fusion.60, s32[]{:T(128)} %constant.191.clone.1, s32[]{:T(128)} %constant.192.clone.1, s32[]{:T(128)} %constant.192.clone.1, s32[]{:T(128)} %constant.192.clone.1) | dynamic-update-slice | bytes 663556 | tf_op jit(solution)/shard_map/scatter | solution.py:90
  90.0 3.3 %add_divide_fusion = f32[1,7,3,8,18,8]{5,4,3,2,1,0:T(8,128)} fusion(f32[1,7,3,8,18,8]{5,4,3,2,1,0:T(8,128)} %slice.507, f32[1,7,3,8,18,8]{5,4,3,2,1,0:T(8,128)S(1)} %slice.509), kind=kLoop, calls=%fused_computation.3 | loop fusion | flops 96768 | bytes 290304 | tf_op jit(solution)/shard_map/div | solution.py:43
  93.4 3.5 %copy.10 = f32[1,7,3,8,18,8]{4,5,3,2,1,0:T(8,128)} copy(f32[1,7,3,8,18,8]{5,4,3,2,1,0:T(8,128)} %add_divide_fusion) | data formatting | bytes 193536 | tf_op jit(solution)/shard_map/div | solution.py:43
  98.6 3.9 %copy.12 = f32[1,8,3,8,18,8]{4,5,3,2,1,0:T(8,128)} copy(f32[1,8,3,8,18,8]{5,4,3,2,1,0:T(8,128)} %stack.44) | data formatting | bytes 221184 | tf_op jit(solution)/shard_map/stack | solution.py:98
  102.5 2.1 %copy.13 = f32[1,8,3,8,18,8]{4,5,3,2,1,0:T(8,128)} copy(f32[1,8,3,8,18,8]{5,4,3,2,1,0:T(8,128)S(1)} %copy-done) | data formatting | bytes 221184 | tf_op jit(solution)/shard_map/stack | solution.py:98
  105.1 2.1 %copy.16 = f32[1,8,3,8,18,8]{4,5,3,2,1,0:T(8,128)} copy(f32[1,8,3,8,18,8]{5,4,3,2,1,0:T(8,128)S(1)} %stack.50) | data formatting | bytes 221184 | tf_op jit(solution)/shard_map/stack | solution.py:91
  107.8 2.1 %copy.15 = f32[1,8,3,8,18,8]{4,5,3,2,1,0:T(8,128)} copy(f32[1,8,3,8,18,8]{5,4,3,2,1,0:T(8,128)S(1)} %stack.49) | data formatting | bytes 221184 | tf_op jit(solution)/shard_map/stack | solution.py:91
  109.8 3.0 %fusion = (f32[3,8,3,18]{3,2,1,0:T(4,128)S(1)}, f32[3,8,3,18]{3,2,1,0:T(4,128)S(1)}) fusion(f32[1,1,3,8,18,8]{4,5,3,2,1,0:T(8,128)S(1)} %copy-done.3, f32[1,7,3,8,18,8]{4,5,3,2,1,0:T(8,128)} %copy.10, f32[1,8,3,8,18,8]{4,5,3,2,1,0:T(8,128)} %copy.13, f32[1,8,3,8,18,8]{4,5,3,2,1,0:T(8,128)} %copy.12, f32[1,8,3,8,18,8]{4,5,3,2,1,0:T(8,128)} %copy.16, ...), kind=kLoop, calls=%fused_computation.1 | loop fusion | flops 743904 | bytes 673920 | tf_op jit(solution)/shard_map/reduce_sum | solution.py:104
  113.2 3.9 %collective-permute-start.4 = (f32[2,3,4,1,18]{4,2,3,1,0:T(4,128)S(1)}, f32[2,3,4,1,18]{4,2,3,1,0:T(4,128)S(1)}, u32[]{:S(2)}, u32[]{:S(2)}) collective-permute-start(f32[2,3,4,1,18]{4,2,3,1,0:T(4,128)S(1)} %get-tuple-element.111), channel_id=1, source_target_pairs={{0,32},{32,64},{64,96},{96,128},{128,160},{160,192},{192,224},{224... | collective-permute-start | bytes 5192 | tf_op jit(solution)/shard_map/ppermute | solution.py:22
  117.1 1.9 %collective-permute-start.5 = (f32[2,3,4,1,18]{4,2,3,1,0:T(4,128)S(1)}, f32[2,3,4,1,18]{4,2,3,1,0:T(4,128)S(1)}, u32[]{:S(2)}, u32[]{:S(2)}) collective-permute-start(f32[2,3,4,1,18]{4,2,3,1,0:T(4,128)S(1)} %get-tuple-element.112), channel_id=1, source_target_pairs={{32,0},{64,32},{96,64},{128,96},{160,128},{192,160},{224,192},{256... | collective-permute-start | bytes 5192 | tf_op jit(solution)/shard_map/ppermute | solution.py:25
  119.1 11.9 %collective-permute-done.5 = f32[2,3,4,1,18]{4,2,3,1,0:T(4,128)S(1)} collective-permute-done((f32[2,3,4,1,18]{4,2,3,1,0:T(4,128)S(1)}, f32[2,3,4,1,18]{4,2,3,1,0:T(4,128)S(1)}, u32[]{:S(2)}, u32[]{:S(2)}) %collective-permute-start.5) | collective-permute-done | bytes 1760 | tf_op jit(solution)/shard_map/ppermute | solution.py:25
  131.1 1.9 %collective-permute-start.6 = (f32[2,3,4,5,1]{4,2,3,1,0:T(4,128)S(1)}, f32[2,3,4,5,1]{4,2,3,1,0:T(4,128)S(1)}, u32[]{:S(2)}, u32[]{:S(2)}) collective-permute-start(f32[2,3,4,5,1]{4,2,3,1,0:T(4,128)S(1)} %get-tuple-element.108), channel_id=1, source_target_pairs={{0,1},{1,2},{2,3},{3,4},{4,5},{5,6},{6,7},{7,8},{8,9},{9,10},{10,1... | collective-permute-start | bytes 1448 | tf_op jit(solution)/shard_map/ppermute | solution.py:22
  133.0 5.5 %collective-permute-start.7 = (f32[2,3,4,5,1]{4,2,3,1,0:T(4,128)S(1)}, f32[2,3,4,5,1]{4,2,3,1,0:T(4,128)S(1)}, u32[]{:S(2)}, u32[]{:S(2)}) collective-permute-start(f32[2,3,4,5,1]{4,2,3,1,0:T(4,128)S(1)} %get-tuple-element.109), channel_id=1, source_target_pairs={{1,0},{2,1},{3,2},{4,3},{5,4},{6,5},{7,6},{8,7},{9,8},{10,9},{11,1... | collective-permute-start | bytes 1448 | tf_op jit(solution)/shard_map/ppermute | solution.py:25
  140.8 5.8 %collective-permute-start.9 = (f32[4,1,1]{2,0,1:T(4,128)S(1)}, f32[4,1,1]{2,0,1:T(4,128)S(1)}, u32[]{:S(2)}, u32[]{:S(2)}) collective-permute-start(f32[4,1,1]{2,0,1:T(4,128)S(1)} %bitcast.79), channel_id=1, source_target_pairs={{1,0},{2,1},{3,2},{4,3},{5,4},{6,5},{7,6},{8,7},{9,8},{10,9},{11,1... | collective-permute-start | bytes 56 | tf_op jit(solution)/shard_map/ppermute | solution.py:33
  146.6 1.9 %collective-permute-start.8 = (f32[4,1,16]{2,0,1:T(4,128)S(1)}, f32[4,1,16]{2,0,1:T(4,128)S(1)}, u32[]{:S(2)}, u32[]{:S(2)}) collective-permute-start(f32[4,1,16]{2,0,1:T(4,128)S(1)} %get-tuple-element.113), channel_id=1, source_target_pairs={{32,0},{64,32},{96,64},{128,96},{160,128},{192,160},{224,192},{256... | collective-permute-start | bytes 776 | tf_op jit(solution)/shard_map/ppermute | solution.py:33
  148.6 11.6 %collective-permute-done.8 = f32[4,1,16]{2,0,1:T(4,128)S(1)} collective-permute-done((f32[4,1,16]{2,0,1:T(4,128)S(1)}, f32[4,1,16]{2,0,1:T(4,128)S(1)}, u32[]{:S(2)}, u32[]{:S(2)}) %collective-permute-start.8) | collective-permute-done | bytes 288 | tf_op jit(solution)/shard_map/ppermute | solution.py:33
  (78 shorter events, 25.5 us)
Async XLA Ops:
  0.6 17.1 %collective-permute-start = (f32[3,8,8,128]{3,2,1,0:T(8,128)}, f32[3,8,8,128]{3,2,1,0:T(8,128)S(1)}, u32[]{:S(2)}, u32[]{:S(2)}) collective-permute-start(f32[3,8,8,128]{3,2,1,0:T(8,128)} %param.14), channel_id=1, source_target_pairs={{0,32},{32,64},{64,96},{96,128},{128,160},{160,192},{192,224},{224... | collective-permute-start | bytes 294920 | tf_op jit(solution)/shard_map/ppermute | solution.py:22
  15.7 16.8 %collective-permute-start.1 = (f32[3,8,8,128]{3,2,1,0:T(8,128)}, f32[3,8,8,128]{3,2,1,0:T(8,128)S(1)}, u32[]{:S(2)}, u32[]{:S(2)}) collective-permute-start(f32[3,8,8,128]{3,2,1,0:T(8,128)} %param.14), channel_id=1, source_target_pairs={{32,0},{64,32},{96,64},{128,96},{160,128},{192,160},{224,192},{256... | collective-permute-start | bytes 294920 | tf_op jit(solution)/shard_map/ppermute | solution.py:25
  33.4 22.0 %collective-permute-start.2 = (f32[3,8,24,8]{3,2,1,0:T(8,128)}, f32[3,8,24,8]{3,2,1,0:T(8,128)}, u32[]{:S(2)}, u32[]{:S(2)}) collective-permute-start(f32[3,8,24,8]{3,2,1,0:T(8,128)} %get-tuple-element.100), channel_id=1, source_target_pairs={{0,1},{1,2},{2,3},{3,4},{4,5},{5,6},{6,7},{7,8},{8,9},{9,10},{10,1... | collective-permute-start | bytes 55304 | tf_op jit(solution)/shard_map/ppermute | solution.py:22
  35.7 19.8 %collective-permute-start.3 = (f32[3,8,24,8]{3,2,1,0:T(8,128)}, f32[3,8,24,8]{3,2,1,0:T(8,128)}, u32[]{:S(2)}, u32[]{:S(2)}) collective-permute-start(f32[3,8,24,8]{3,2,1,0:T(8,128)} %get-tuple-element.101), channel_id=1, source_target_pairs={{1,0},{2,1},{3,2},{4,3},{5,4},{6,5},{7,6},{8,7},{9,8},{10,9},{11,1... | collective-permute-start | bytes 55304 | tf_op jit(solution)/shard_map/ppermute | solution.py:25
  71.9 16.3 %copy-start.2 = (f32[1,7,24,144]{3,2,1,0:T(8,128)S(1)}, f32[1,7,24,144]{3,2,1,0:T(8,128)}, u32[]{:S(2)}) copy-start(f32[1,7,24,144]{3,2,1,0:T(8,128)} %get-tuple-element.96) | copy-start | bytes 290308
  93.4 3.5 %copy-start.1 = (f32[1,8,24,144]{3,2,1,0:T(8,128)S(1)}, f32[1,8,24,144]{3,2,1,0:T(8,128)}, u32[]{:S(2)}) copy-start(f32[1,8,24,144]{3,2,1,0:T(8,128)} %get-tuple-element.89) | copy-start | bytes 331780
  98.6 3.9 %copy-start = (f32[1,8,3,8,18,8]{5,4,3,2,1,0:T(8,128)S(1)}, f32[1,8,3,8,18,8]{5,4,3,2,1,0:T(8,128)}, u32[]{:S(2)}) copy-start(f32[1,8,3,8,18,8]{5,4,3,2,1,0:T(8,128)} %stack.45) | copy-start | bytes 331780
  107.2 2.6 %copy-start.3 = (f32[1,1,3,8,18,8]{4,5,3,2,1,0:T(8,128)S(1)}, f32[1,1,3,8,18,8]{4,5,3,2,1,0:T(8,128)}, u32[]{:S(2)}) copy-start(f32[1,1,3,8,18,8]{4,5,3,2,1,0:T(8,128)} %copy.11) | copy-start | bytes 41476
  109.8 3.0 %copy-start.5 = (s32[8]{0:T(128)S(1)}, s32[8]{0:T(128)}, u32[]{:S(2)}) copy-start(s32[8]{0:T(128)} %param.15) | copy-start | bytes 100
  113.2 5.8 %collective-permute-start.4 = (f32[2,3,4,1,18]{4,2,3,1,0:T(4,128)S(1)}, f32[2,3,4,1,18]{4,2,3,1,0:T(4,128)S(1)}, u32[]{:S(2)}, u32[]{:S(2)}) collective-permute-start(f32[2,3,4,1,18]{4,2,3,1,0:T(4,128)S(1)} %get-tuple-element.111), channel_id=1, source_target_pairs={{0,32},{32,64},{64,96},{96,128},{128,160},{160,192},{192,224},{224... | collective-permute-start | bytes 5192 | tf_op jit(solution)/shard_map/ppermute | solution.py:22
  117.1 13.8 %collective-permute-start.5 = (f32[2,3,4,1,18]{4,2,3,1,0:T(4,128)S(1)}, f32[2,3,4,1,18]{4,2,3,1,0:T(4,128)S(1)}, u32[]{:S(2)}, u32[]{:S(2)}) collective-permute-start(f32[2,3,4,1,18]{4,2,3,1,0:T(4,128)S(1)} %get-tuple-element.112), channel_id=1, source_target_pairs={{32,0},{64,32},{96,64},{128,96},{160,128},{192,160},{224,192},{256... | collective-permute-start | bytes 5192 | tf_op jit(solution)/shard_map/ppermute | solution.py:25
  131.1 7.4 %collective-permute-start.6 = (f32[2,3,4,5,1]{4,2,3,1,0:T(4,128)S(1)}, f32[2,3,4,5,1]{4,2,3,1,0:T(4,128)S(1)}, u32[]{:S(2)}, u32[]{:S(2)}) collective-permute-start(f32[2,3,4,5,1]{4,2,3,1,0:T(4,128)S(1)} %get-tuple-element.108), channel_id=1, source_target_pairs={{0,1},{1,2},{2,3},{3,4},{4,5},{5,6},{6,7},{7,8},{8,9},{9,10},{10,1... | collective-permute-start | bytes 1448 | tf_op jit(solution)/shard_map/ppermute | solution.py:22
  133.0 6.8 %collective-permute-start.7 = (f32[2,3,4,5,1]{4,2,3,1,0:T(4,128)S(1)}, f32[2,3,4,5,1]{4,2,3,1,0:T(4,128)S(1)}, u32[]{:S(2)}, u32[]{:S(2)}) collective-permute-start(f32[2,3,4,5,1]{4,2,3,1,0:T(4,128)S(1)} %get-tuple-element.109), channel_id=1, source_target_pairs={{1,0},{2,1},{3,2},{4,3},{5,4},{6,5},{7,6},{8,7},{9,8},{10,9},{11,1... | collective-permute-start | bytes 1448 | tf_op jit(solution)/shard_map/ppermute | solution.py:25
  140.7 20.2 %copy-start.4 = (f32[1,3,4,1,16]{4,2,3,1,0:T(4,128)}, f32[1,3,4,1,16]{4,2,3,1,0:T(4,128)S(1)}, u32[]{:S(2)}) copy-start(f32[1,3,4,1,16]{4,2,3,1,0:T(4,128)S(1)} %fusion.78) | copy-start | bytes 2308
  140.8 7.7 %collective-permute-start.9 = (f32[4,1,1]{2,0,1:T(4,128)S(1)}, f32[4,1,1]{2,0,1:T(4,128)S(1)}, u32[]{:S(2)}, u32[]{:S(2)}) collective-permute-start(f32[4,1,1]{2,0,1:T(4,128)S(1)} %bitcast.79), channel_id=1, source_target_pairs={{1,0},{2,1},{3,2},{4,3},{5,4},{6,5},{7,6},{8,7},{9,8},{10,9},{11,1... | collective-permute-start | bytes 56 | tf_op jit(solution)/shard_map/ppermute | solution.py:33
  146.6 13.6 %collective-permute-start.8 = (f32[4,1,16]{2,0,1:T(4,128)S(1)}, f32[4,1,16]{2,0,1:T(4,128)S(1)}, u32[]{:S(2)}, u32[]{:S(2)}) collective-permute-start(f32[4,1,16]{2,0,1:T(4,128)S(1)} %get-tuple-element.113), channel_id=1, source_target_pairs={{32,0},{64,32},{96,64},{128,96},{160,128},{192,160},{224,192},{256... | collective-permute-start | bytes 776 | tf_op jit(solution)/shard_map/ppermute | solution.py:33
where the time goes:
time: 161 us
  local copies, waits for them, and re-layouts  56.8 us (35%)
  starting transfers between devices  45.5 us (28%)
  waiting for transfers between devices  38.7 us (24%)
  other arithmetic  18.5 us (11%)
    ppermute x4, waiting for transfers between devices, with_halo(): lax.ppermute(lax.slice_in_dim(block, 0, width, axis=dim), axis, backward)  27.1 us
    ppermute x4, starting transfers between devices, with_halo(): lax.ppermute(lax.slice_in_dim(block, block.shape[dim] - width, None, axis...  23.1 us
    ppermute x4, starting transfers between devices, with_halo(): lax.ppermute(lax.slice_in_dim(block, 0, width, axis=dim), axis, backward)  14.7 us
    scatter x1, local copies, waits for them, and re-layouts, patch_partials(): full = ghost.at[:, 1:-1, 1:-1, 1:-1].set(pressure)  13.7 us
    scatter x1, local copies, waits for them, and re-layouts, patch_partials(): boundary = inflow_of(ghost.at[:, 1:-1, 1:-1, 1:-1].set(0.0))  13.7 us
    ppermute x2, waiting for transfers between devices, shifted(): lax.ppermute(value, axis, [(source, source + steps) for source in range(i...  11.6 us
    another operation x4, local copies, waits for them, and re-layouts, patch_partials(): faces = jnp.stack([tx[:, 1:], ty[:, :, 1:], tz[1:]])  9.92 us
    ppermute x2, starting transfers between devices, shifted(): lax.ppermute(value, axis, [(source, source + steps) for source in range(i...  7.71 us
  transfers between devices with their start and end apart: 10, of which 4 were waited for; matrix products, arithmetic and copies ran while one was open for 10% of the time, Pallas kernels for 0%

commit v1 on v0

v1 whole, which is shorter than its diff:
```python
import math

import jax
import jax.numpy as jnp
from jax import lax
from jax.experimental import pallas as pl
from jax.experimental.pallas import tpu as pltpu
from jax.sharding import PartitionSpec as P

MESH = pl.DeviceIdType.MESH
NCL = 4
BXY = 8
SWEEPS = 4
KMIN = 0.01
EPS = 1e-06
NZ = 8
LANES = 128
F32 = jnp.float32

DOWN = [(1, r) for r in range(4)] + [(2, r) for r in range(4)] + [(0, r) for r in range(5)]
UP = [(0, r) for r in range(4, 8)] + [(1, r) for r in range(5, 8)] + [(2, r) for r in range(5, 8)]
PLANES = DOWN + UP[1:] + [(1, 4), (2, 4)]
PLANE_AT = {cr: at for at, cr in enumerate(PLANES)}
UP_FROM = PLANE_AT[UP[0]]
SLOT = 9
PACKS = [DOWN, UP + [(1, 4), (2, 4)]]
DIRECTIONS = [(1, 0), (-1, 0), (1, 1), (1, -1), (-1, 1), (-1, -1), (0, 1), (0, -1)]
LEFT_AT = 20
RIGHT_AT = 72
W = [1.0 / (1.05 + 0.95 * math.cos(math.pi * (2 * s + 1) / (2 * SWEEPS))) for s in range(SWEEPS)]


def harmonic(left, right):
    return 2.0 * left * right / (left + right)


def lane_of(shape):
    return lax.broadcasted_iota(jnp.int32, shape, len(shape) - 1)


def between(lane, low, high):
    return (lane >= low) & (lane < high)


def kernel(
    n_gx, n_gy, k_hbm, map_hbm, perm_ref, trans_ref,
    k_own, map_own, planes, packs, from_low, from_high, packs_own, packs_low, packs_high,
    kp, coef, face, q1, q2, q3, q4, u_coef, uq, mess, mess_x, mess_y,
    load_sem, send_sem, recv_sem,
):
    i, j = lax.axis_index("gx"), lax.axis_index("gy")
    load_k = pltpu.make_async_copy(k_hbm, k_own, load_sem.at[0])
    load_map = pltpu.make_async_copy(map_hbm, map_own, load_sem.at[1])
    load_k.start()
    load_map.start()

    def inside(di, dj):
        tests = []
        if di:
            tests.append(i + di < n_gx if di > 0 else i >= -di)
        if dj:
            tests.append(j + dj < n_gy if dj > 0 else j >= -dj)
        return tests[0] if len(tests) == 1 else tests[0] & tests[1]

    def device(di, dj):
        return {"gx": i + di, "gy": j + dj}

    barrier = pltpu.get_barrier_semaphore()
    for di, dj in DIRECTIONS:
        @pl.when(inside(di, dj))
        def _():
            pl.semaphore_signal(barrier, inc=1, device_id=device(di, dj), device_id_type=MESH)

    lane = lane_of((NZ, LANES))
    load_k.wait()
    packed = [jnp.zeros((NZ, LANES), F32), jnp.zeros((NZ, LANES), F32)]
    for at, (c, r) in enumerate(PLANES):
        plane = k_own[pl.ds(c * 64 + r, NZ, stride=8), :]
        planes[at] = plane
        for v, pack in enumerate(PACKS):
            if (c, r) in pack:
                s = SLOT * pack.index((c, r))
                packed[v] = jnp.where(between(lane, s, s + SLOT), pltpu.roll(plane, s + 4, axis=1), packed[v])
    packs[0] = packed[0]
    packs[1] = packed[1]

    rows_near = 1 + (i > 0).astype(jnp.int32) + (i < n_gx - 1).astype(jnp.int32)
    cols_near = 1 + (j > 0).astype(jnp.int32) + (j < n_gy - 1).astype(jnp.int32)
    pl.semaphore_wait(barrier, rows_near * cols_near - 1)

    def copy_of(k, di, dj):
        side = 0 if dj > 0 else 1
        if dj == 0:
            if di > 0:
                source, target = planes.at[pl.ds(UP_FROM, len(UP))], from_low
            else:
                source, target = planes.at[pl.ds(0, len(DOWN))], from_high
        elif di == 0:
            source, target = packs, packs_own.at[side]
        elif di > 0:
            source, target = packs.at[1], packs_low.at[side]
        else:
            source, target = packs.at[0], packs_high.at[side]
        return pltpu.make_async_remote_copy(
            src_ref=source, dst_ref=target, send_sem=send_sem.at[k], recv_sem=recv_sem.at[k],
            device_id=device(di, dj), device_id_type=MESH,
        )

    copies = []
    for k, (di, dj) in enumerate(DIRECTIONS):
        copy = copy_of(k, di, dj)
        copies.append(copy)
        pl.when(inside(di, dj))(copy.start)

    def arrive(k, di, dj):
        copy, target = copies[k], copy_of(k, di, dj).dst_ref
        here = inside(-di, -dj)
        pl.when(here)(copy.wait_recv)

        @pl.when(jnp.logical_not(here))
        def _():
            target[...] = jnp.zeros(target.shape, F32)

    edge = (lane >= LANES - 4) | (lane < 5)
    slot_left = lax.rem(lane, SLOT) < 4

    def assemble(c, r, merged):
        if 0 <= r < 8:
            own = planes[PLANE_AT[c, r]]
            v = 0 if (c, r) in DOWN else 1
            s = SLOT * PACKS[v].index((c, r))
            pack = merged[v]
        elif r < 0:
            at = UP.index((c, r + 8))
            own, s, pack = from_low[at], SLOT * at, merged
        else:
            at = DOWN.index((c, r - 8))
            own, s, pack = from_high[at], SLOT * at, merged
        margin = pltpu.roll(pack, (2 * LANES - s - 4) % LANES, axis=1)
        left = pltpu.roll(jnp.where(lane >= LANES - 4, margin, own), LEFT_AT + 4, axis=1)
        right = pltpu.roll(jnp.where(lane < 5, margin, own), RIGHT_AT + 8, axis=1)
        other = jnp.where(between(lane, LEFT_AT, LEFT_AT + 12), left, 1.0)
        other = jnp.where(between(lane, RIGHT_AT, RIGHT_AT + 13), right, other)
        other = jnp.where(edge, margin, other)
        kp[c, r + 4, :, 0:LANES] = own + KMIN
        kp[c, r + 4, :, LANES : 2 * LANES] = other + KMIN

    lane2 = lane_of((1, NZ, 2 * LANES))
    layer2 = lax.broadcasted_iota(jnp.int32, (1, NZ, 2 * LANES), 1)
    left_end = lane2 == LANES + LEFT_AT + 11
    right_start = lane2 == LANES + RIGHT_AT
    top, bottom = layer2 == NZ - 1, layer2 == 0
    zero = jnp.zeros((1, NZ, 2 * LANES), F32)

    def y_next(v):
        return pltpu.roll(v, 2 * LANES - 1, axis=2)

    def y_last(v):
        return pltpu.roll(v, 1, axis=2)

    def z_next(v):
        return pltpu.roll(v, NZ - 1, axis=1)

    def z_last(v):
        return pltpu.roll(v, 1, axis=1)

    def finish(tx_low, tx_high, ty_low, ty_high, tz_low, tz_high, low_end, high_end):
        inverse = 1.0 / (tx_low + tx_high + ty_low + ty_high + tz_low + tz_high)
        return [
            zero if low_end else tx_low * inverse,
            zero if high_end else tx_high * inverse,
            jnp.where(right_start, 0.0, ty_low * inverse),
            jnp.where(left_end, 0.0, ty_high * inverse),
            jnp.where(bottom, 0.0, tz_low * inverse),
            jnp.where(top, 0.0, tz_high * inverse),
            (tx_high - tx_low) * inverse,
            (ty_high - ty_low) * inverse,
            (tz_high - tz_low) * inverse,
        ]

    def coefficients(r):
        kx_low, kx, kx_high = (kp[0, pl.ds(r + 4 + d, 1)] for d in (-1, 0, 1))
        ky, kz = kp[1, pl.ds(r + 4, 1)], kp[2, pl.ds(r + 4, 1)]
        tx_low, tx_high = harmonic(kx_low, kx), harmonic(kx, kx_high)
        ty = harmonic(ky, y_next(ky))
        ty_low = jnp.where(right_start, ky, y_last(ty))
        ty_high = jnp.where(left_end, ky, ty)
        tz = harmonic(kz, z_next(kz))
        tz_low = jnp.where(bottom, kz, z_last(tz))
        tz_high = jnp.where(top, kz, tz)
        for n, value in enumerate(finish(tx_low, tx_high, ty_low, ty_high, tz_low, tz_high, False, False)):
            coef[n, pl.ds(r + 3, 1)] = value
            if n >= 6:
                q1[n - 6, pl.ds(r + 3, 1)] = W[0] * value
        if 0 <= r < 8:
            for d, value in enumerate((tx_high, ty_high, tz_high)):
                face[d, pl.ds(r, 1)] = value
        if r == 0 or r == 7:
            e = 0 if r == 0 else 1
            low, high = (kx, tx_high) if r == 0 else (tx_low, kx)
            for n, value in enumerate(finish(low, high, ty_low, ty_high, tz_low, tz_high, r == 0, r == 7)):
                u_coef[e, pl.ds(n, 1)] = value
                if n >= 6:
                    uq[e, 0, n - 6, pl.ds(0, 1)] = W[0] * value

    def sweep(w, cs, low, mid, high):
        around = cs[2] * y_last(mid) + cs[3] * y_next(mid) + cs[4] * z_last(mid) + cs[5] * z_next(mid)
        if low is not None:
            around = around + cs[0] * low
        if high is not None:
            around = around + cs[1] * high
        return mid + w * (around + cs[6] - mid)

    def coefs_at(r, d):
        return [coef[n, pl.ds(r + 3, 1)] for n in (0, 1, 2, 3, 4, 5, 6 + d)]

    qs = [(q1, 3), (q2, 2), (q3, 1), (q4, 0)]

    def q_at(s, d, r):
        ref, offset = qs[s]
        return ref[d, pl.ds(r + offset, 1)]

    def e_at(e, s, d, n):
        r = n if e == 0 else 7 - n
        return uq[e, s, d, pl.ds(n, 1)] if n <= s else q_at(s, d, r)

    def main_row(s, r):
        for d in range(3):
            low, mid, high = (q_at(s - 1, d, r + n) for n in (-1, 0, 1))
            ref, offset = qs[s]
            ref[d, pl.ds(r + offset, 1)] = sweep(W[s], coefs_at(r, d), low, mid, high)

    def edge_row(e, s, n):
        r = n if e == 0 else 7 - n
        for d in range(3):
            inner, mid = e_at(e, s - 1, d, n + 1), e_at(e, s - 1, d, n)
            outer = e_at(e, s - 1, d, n - 1) if n else None
            cs = coefs_at(r, d) if n else [u_coef[e, pl.ds(m, 1)] for m in (0, 1, 2, 3, 4, 5, 6 + d)]
            low, high = (outer, inner) if e == 0 else (inner, outer)
            uq[e, s, d, pl.ds(n, 1)] = sweep(W[s], cs, low, mid, high)

    for k in (6, 7):
        arrive(k, *DIRECTIONS[k])
    merged = [jnp.where(slot_left, packs_own[0, v], packs_own[1, v]) for v in range(2)]
    for r in range(8):
        for c in range(3):
            assemble(c, r, merged)
    for r in range(1, 7):
        coefficients(r)

    for k in (2, 3, 0):
        arrive(k, *DIRECTIONS[k])
    merged = jnp.where(slot_left, packs_low[0], packs_low[1])
    for r in range(-4, 0):
        for c in range(3):
            if r > -4 or c == 0:
                assemble(c, r, merged)
    for r in range(-3, 1):
        coefficients(r)
    for k in (4, 5, 1):
        arrive(k, *DIRECTIONS[k])
    merged = jnp.where(slot_left, packs_high[0], packs_high[1])
    for r in range(8, 13):
        for c in range(3):
            if r < 12 or c == 0:
                assemble(c, r, merged)
    for r in range(7, 12):
        coefficients(r)

    for s in range(1, SWEEPS):
        for r in range(s - 4 + 1, 12 - s):
            main_row(s, r)
        for e in range(2):
            for n in range(s + 1):
                edge_row(e, s, n)

    sums = []
    flag_up = (i < n_gx - 1).astype(F32)
    flag_low = (i > 0).astype(F32)
    last = SWEEPS - 1

    def drop(d, here, above):
        if d == 0:
            return here - above - 1.0
        if d == 1:
            return here - jnp.where(left_end, 0.0, y_next(here)) - 1.0
        return here - jnp.where(top, 0.0, z_next(here)) - 1.0

    energies, squares = [], []
    for d in range(3):
        def terms(r, here, above, at_end=False):
            fall = drop(d, here, above)
            square = fall * fall
            t = kp[0, pl.ds(r + 4, 1)] if at_end else face[d, pl.ds(r, 1)]
            return jnp.concatenate([t * square, square], axis=0)

        main = [terms(r, q_at(last, d, r), q_at(last, d, r + 1) if d == 0 else None) for r in range(8)]
        up = [terms(r, e_at(0, last, d, r), e_at(0, last, d, r + 1)) for r in range(4)]
        low = [
            terms(r, e_at(1, last, d, 7 - r), zero if r == 7 else e_at(1, last, d, 6 - r), d == 0 and r == 7)
            for r in range(4, 8)
        ]
        third = terms(3, e_at(1, last, d, 4), e_at(1, last, d, 3)) if d == 0 else main[3]
        main_low = main[0] + main[1] + main[2]
        main_high = main[4] + main[5] + main[6] + main[7]
        total = main_low + main[3] + main_high
        total = total + flag_up * (up[0] + up[1] + up[2] + up[3] + main_high)
        total = total + flag_low * (main_low + third + low[0] + low[1] + low[2] + low[3])
        own, other = total[:, :, 0:LANES], total[:, :, LANES : 2 * LANES]
        lane3 = lane_of(own.shape)
        flag_left = (j > 0).astype(F32)
        flag_right = (j < n_gy - 1).astype(F32)
        left = pltpu.roll(other, LANES - LEFT_AT - 4, axis=2) * flag_left
        right = pltpu.roll(other, LANES - RIGHT_AT - 8, axis=2) * flag_right
        own = own + jnp.where(lane3 < 8, left, 0.0) + jnp.where(lane3 >= LANES - 8, right, 0.0)
        sums.append(own)
    stack = jnp.concatenate(sums, axis=0).reshape(6 * NZ, LANES)
    pick = (lax.broadcasted_iota(jnp.int32, (LANES, LANES), 0) // BXY == lane_of((LANES, LANES))).astype(F32)
    blocks = jnp.dot(stack, pick, precision=lax.Precision.HIGHEST, preferred_element_type=F32)
    blocks = blocks.reshape(3, 2, NZ, LANES)

    load_map.wait()
    layer = lax.broadcasted_iota(jnp.int32, (NZ, LANES), 0)
    layer_map = jnp.zeros((NZ, LANES), jnp.int32)
    for z in range(NZ):
        layer_map = jnp.where(layer == z, map_own[z], layer_map)
    extents = (24, 144, 8)
    perm = [[None] * NCL for _ in range(3)]
    for n in range(NCL):
        for d in range(3):
            held = jnp.where(layer_map == n, blocks[d], 0.0)
            both = jnp.sum(held, axis=1, keepdims=True)
            perm[d][n] = both[0] / (both[1] + EPS * extents[d] * extents[d])
    mess[...] = jnp.concatenate(perm[0] + perm[1], axis=0)

    def tell(k, di, dj, target):
        return pltpu.make_async_remote_copy(
            src_ref=mess, dst_ref=target, send_sem=send_sem.at[k], recv_sem=recv_sem.at[k],
            device_id=device(di, dj), device_id_type=MESH,
        )

    last_copies = [(8, -1, 0, mess_x), (9, 0, -1, mess_y)]
    for k, di, dj, target in last_copies:
        pl.when(inside(di, dj))(tell(k, di, dj, target).start)
    for d in range(3):
        for n in range(NCL):
            perm_ref[d, n] = perm[d][n][:, 0 : LANES // BXY]
    for n in range(NCL):
        value = harmonic(perm[2][n], perm[2][n + 1]) if n < NCL - 1 else jnp.zeros((1, LANES), F32)
        trans_ref[2, n] = value[:, 0 : LANES // BXY]
    for k, (di, dj) in enumerate(DIRECTIONS):
        pl.when(inside(di, dj))(copies[k].wait_send)
    for k, di, dj, target in last_copies:
        copy, here = tell(k, di, dj, target), inside(-di, -dj)
        pl.when(here)(copy.wait_recv)

        @pl.when(jnp.logical_not(here))
        def _():
            target[...] = jnp.zeros(target.shape, F32)

    lane1 = lane_of((1, LANES))
    for n in range(NCL):
        trans_ref[0, n] = harmonic(perm[0][n], mess_x[pl.ds(n, 1)])[:, 0 : LANES // BXY]
        beyond = pltpu.roll(mess_y[pl.ds(NCL + n, 1)], LANES // BXY - 1, axis=1)
        after = jnp.where(lane1 == LANES // BXY - 1, beyond, pltpu.roll(perm[1][n], LANES - 1, axis=1))
        trans_ref[1, n] = harmonic(perm[1][n], after)[:, 0 : LANES // BXY]
    for k, di, dj, target in last_copies:
        pl.when(inside(di, dj))(tell(k, di, dj, target).wait_send)


def solution(mesh):
    n_gx, n_gy = mesh.shape["gx"], mesh.shape["gy"]

    def local(permeability, layer_map):
        k = permeability.reshape(3 * NZ * BXY, LANES)
        out = jax.ShapeDtypeStruct((3, NCL, 1, LANES // BXY), F32)
        vmem = lambda *shape: pltpu.VMEM(shape, F32)
        both = 2 * LANES
        return pl.pallas_call(
            lambda *refs: kernel(n_gx, n_gy, *refs),
            out_shape=(out, out),
            in_specs=[pl.BlockSpec(memory_space=pl.ANY)] * 2,
            out_specs=(pl.BlockSpec(memory_space=pltpu.VMEM),) * 2,
            scratch_shapes=[
                vmem(3 * NZ * BXY, LANES),
                pltpu.SMEM((NZ,), jnp.int32),
                vmem(len(PLANES), NZ, LANES),
                vmem(2, NZ, LANES),
                vmem(len(UP), NZ, LANES),
                vmem(len(DOWN), NZ, LANES),
                vmem(2, 2, NZ, LANES),
                vmem(2, NZ, LANES),
                vmem(2, NZ, LANES),
                vmem(3, 17, NZ, both),
                vmem(9, 15, NZ, both),
                vmem(3, 8, NZ, both),
                vmem(3, 15, NZ, both),
                vmem(3, 13, NZ, both),
                vmem(3, 11, NZ, both),
                vmem(3, 9, NZ, both),
                vmem(2, 9, NZ, both),
                vmem(2, SWEEPS, 3, SWEEPS, NZ, both),
                vmem(NZ, LANES),
                vmem(NZ, LANES),
                vmem(NZ, LANES),
                pltpu.SemaphoreType.DMA((2,)),
                pltpu.SemaphoreType.DMA((10,)),
                pltpu.SemaphoreType.DMA((10,)),
            ],
            compiler_params=pltpu.CompilerParams(collective_id=0, has_side_effects=True),
            name="upscale",
        )(k, layer_map)

    spec = P(None, None, "gx", "gy")
    return jax.shard_map(local, mesh=mesh, in_specs=(spec, P()), out_specs=(spec, spec), check_vma=False)
```

time: 161 us -> 36.5 us (0.23)
  the two profiles are of different devices: /device:TPU:57 before, /device:TPU:1 now
where the time goes in v1:
time: 36.5 us; the launch traced here: 36.3 us
  Pallas kernels  33.8 us (93%)
  local copies, waits for them, and re-layouts  1.89 us (5%)
  between operations  0.65 us (2%)
    pallas_call x1, Pallas kernels, local(): pl.pallas_call(lambda *refs: kernel(n_gx, n_gy, *refs), out_shape=(out, o...  33.8 us
    unnamed x4, local copies, waits for them, and re-layouts  1.89 us

profile of v1, /device:TPU:1, one launch (start us, length us, event | category | flops | bytes accessed | tf_op | source)
XLA Modules:
  0.0 36.3 jit_solution(12757814145119991482)
XLA Ops:
  0.6 33.8 %upscale.1 = (f32[3,4,1,16]{3,2,1,0:T(1,128)}, f32[3,4,1,16]{3,2,1,0:T(1,128)}) custom-call(f32[192,128]{1,0:T(8,128)} %bitcast.1, s32[8]{0:T(128)} %refs_1_.1), custom_call_target="tpu_custom_call" | custom-call | tf_op jit(solution)/shard_map/upscale/pallas_call | solution.py:379
  34.4 0.0 copy-start
  34.4 1.3 %copy.6 = f32[3,4,1,16]{3,2,1,0:T(1,128)} copy(f32[3,4,1,16]{3,2,1,0:T(1,128)} %get-tuple-element.4) | data formatting | bytes 1536
  35.7 0.0 copy-done
  35.7 0.6 %copy.7 = f32[3,4,1,16]{3,2,1,0:T(1,128)} copy(f32[3,4,1,16]{3,2,1,0:T(1,128)S(1)} %copy-done) | data formatting | bytes 1536
Async XLA Ops:
  34.4 1.3 %copy-start = (f32[3,4,1,16]{3,2,1,0:T(1,128)S(1)}, f32[3,4,1,16]{3,2,1,0:T(1,128)}, u32[]{:S(2)}) copy-start(f32[3,4,1,16]{3,2,1,0:T(1,128)} %get-tuple-element.5) | copy-start | bytes 2308

commit v2 on v1

--- a/solution.py
+++ b/solution.py
@@ -25,6 +25,8 @@
 SLOT = 9
 PACKS = [DOWN, UP + [(1, 4), (2, 4)]]
 DIRECTIONS = [(1, 0), (-1, 0), (1, 1), (1, -1), (-1, 1), (-1, -1), (0, 1), (0, -1)]
+MORE = [(-1, 0), (-1, 1), (-1, -1), (-2, 0), (-2, 1), (-2, -1)]
+ENDS = [0, 7, 8, 15]
 LEFT_AT = 20
 RIGHT_AT = 72
 W = [1.0 / (1.05 + 0.95 * math.cos(math.pi * (2 * s + 1) / (2 * SWEEPS))) for s in range(SWEEPS)]
@@ -45,6 +47,7 @@
 def kernel(
     n_gx, n_gy, k_hbm, map_hbm, perm_ref, trans_ref,
     k_own, map_own, planes, packs, from_low, from_high, packs_own, packs_low, packs_high,
+    more_high, far_high, packs_more, packs_far,
     kp, coef, face, q1, q2, q3, q4, u_coef, uq, mess, mess_x, mess_y,
     load_sem, send_sem, recv_sem,
 ):
@@ -65,11 +68,24 @@
     def device(di, dj):
         return {"gx": i + di, "gy": j + dj}
 
+    def reaches(di, dj):
+        row, col = i + di, j + dj
+        early = jnp.where(col < n_gy // 2, 1, 3)
+        return (lax.rem(row + 4, 4) == early) & (row + 1 < n_gx)
+
     barrier = pltpu.get_barrier_semaphore()
     for di, dj in DIRECTIONS:
         @pl.when(inside(di, dj))
         def _():
             pl.semaphore_signal(barrier, inc=1, device_id=device(di, dj), device_id_type=MESH)
+
+    signals = 0
+    for di, dj in MORE[3:]:
+        @pl.when(inside(-di, -dj) & reaches(0, 0))
+        def _():
+            pl.semaphore_signal(barrier, inc=1, device_id=device(-di, -dj), device_id_type=MESH)
+
+        signals = signals + (inside(di, dj) & reaches(di, dj)).astype(jnp.int32)
 
     lane = lane_of((NZ, LANES))
     load_k.wait()
@@ -86,7 +102,7 @@
 
     rows_near = 1 + (i > 0).astype(jnp.int32) + (i < n_gx - 1).astype(jnp.int32)
     cols_near = 1 + (j > 0).astype(jnp.int32) + (j < n_gy - 1).astype(jnp.int32)
-    pl.semaphore_wait(barrier, rows_near * cols_near - 1)
+    pl.semaphore_wait(barrier, rows_near * cols_near - 1 + signals)
 
     def copy_of(k, di, dj):
         side = 0 if dj > 0 else 1
@@ -106,15 +122,32 @@
             device_id=device(di, dj), device_id_type=MESH,
         )
 
-    copies = []
-    for k, (di, dj) in enumerate(DIRECTIONS):
-        copy = copy_of(k, di, dj)
-        copies.append(copy)
-        pl.when(inside(di, dj))(copy.start)
-
-    def arrive(k, di, dj):
-        copy, target = copies[k], copy_of(k, di, dj).dst_ref
-        here = inside(-di, -dj)
+    def more_of(k, di, dj):
+        side = 0 if dj > 0 else 1
+        if dj == 0:
+            if di == -1:
+                source, target = planes.at[pl.ds(len(DOWN), len(PLANES) - len(DOWN))], more_high
+            else:
+                source, target = planes.at[pl.ds(0, len(DOWN))], far_high
+        elif di == -1:
+            source, target = packs.at[1], packs_more.at[side]
+        else:
+            source, target = packs.at[0], packs_far.at[side]
+        return pltpu.make_async_remote_copy(
+            src_ref=source, dst_ref=target, send_sem=send_sem.at[k], recv_sem=recv_sem.at[k],
+            device_id=device(di, dj), device_id_type=MESH,
+        )
+
+    copies = [(copy_of(k, *to), inside(*to), inside(-to[0], -to[1])) for k, to in enumerate(DIRECTIONS)]
+    for k, (di, dj) in enumerate(MORE):
+        sends = inside(di, dj) & reaches(di, dj)
+        copies.append((more_of(len(DIRECTIONS) + k, di, dj), sends, inside(-di, -dj)))
+    for copy, sends, _ in copies:
+        pl.when(sends)(copy.start)
+
+    def arrive(k):
+        copy, _, here = copies[k]
+        target = copy.dst_ref
         pl.when(here)(copy.wait_recv)
 
         @pl.when(jnp.logical_not(here))
@@ -133,9 +166,12 @@
         elif r < 0:
             at = UP.index((c, r + 8))
             own, s, pack = from_low[at], SLOT * at, merged
+        elif r >= 16 or (c, r - 8) in DOWN:
+            at = DOWN.index((c, r % 8))
+            own, s, pack = (from_high if r < 16 else far_high)[at], SLOT * at, merged
         else:
-            at = DOWN.index((c, r - 8))
-            own, s, pack = from_high[at], SLOT * at, merged
+            at = PLANE_AT[c, r - 8] - len(DOWN)
+            own, s, pack = more_high[at], SLOT * PACKS[1].index((c, r - 8)), merged
         margin = pltpu.roll(pack, (2 * LANES - s - 4) % LANES, axis=1)
         left = pltpu.roll(jnp.where(lane >= LANES - 4, margin, own), LEFT_AT + 4, axis=1)
         right = pltpu.roll(jnp.where(lane < 5, margin, own), RIGHT_AT + 8, axis=1)
@@ -192,13 +228,14 @@
             coef[n, pl.ds(r + 3, 1)] = value
             if n >= 6:
                 q1[n - 6, pl.ds(r + 3, 1)] = W[0] * value
-        if 0 <= r < 8:
+        if 0 <= r < 16:
             for d, value in enumerate((tx_high, ty_high, tz_high)):
-                face[d, pl.ds(r, 1)] = value
-        if r == 0 or r == 7:
-            e = 0 if r == 0 else 1
-            low, high = (kx, tx_high) if r == 0 else (tx_low, kx)
-            for n, value in enumerate(finish(low, high, ty_low, ty_high, tz_low, tz_high, r == 0, r == 7)):
+                if r < 8 or d == 0:
+                    face[d, pl.ds(r, 1)] = value
+        if r in ENDS:
+            e = ENDS.index(r)
+            low, high = (tx_low, kx) if e % 2 else (kx, tx_high)
+            for n, value in enumerate(finish(low, high, ty_low, ty_high, tz_low, tz_high, not e % 2, e % 2)):
                 u_coef[e, pl.ds(n, 1)] = value
                 if n >= 6:
                     uq[e, 0, n - 6, pl.ds(0, 1)] = W[0] * value
@@ -221,26 +258,26 @@
         return ref[d, pl.ds(r + offset, 1)]
 
     def e_at(e, s, d, n):
-        r = n if e == 0 else 7 - n
+        r = ENDS[e] - n if e % 2 else ENDS[e] + n
         return uq[e, s, d, pl.ds(n, 1)] if n <= s else q_at(s, d, r)
 
-    def main_row(s, r):
-        for d in range(3):
+    def main_row(s, r, along=range(3)):
+        for d in along:
             low, mid, high = (q_at(s - 1, d, r + n) for n in (-1, 0, 1))
             ref, offset = qs[s]
             ref[d, pl.ds(r + offset, 1)] = sweep(W[s], coefs_at(r, d), low, mid, high)
 
-    def edge_row(e, s, n):
-        r = n if e == 0 else 7 - n
-        for d in range(3):
+    def edge_row(e, s, n, along=range(3)):
+        r = ENDS[e] - n if e % 2 else ENDS[e] + n
+        for d in along:
             inner, mid = e_at(e, s - 1, d, n + 1), e_at(e, s - 1, d, n)
             outer = e_at(e, s - 1, d, n - 1) if n else None
             cs = coefs_at(r, d) if n else [u_coef[e, pl.ds(m, 1)] for m in (0, 1, 2, 3, 4, 5, 6 + d)]
-            low, high = (outer, inner) if e == 0 else (inner, outer)
+            low, high = (inner, outer) if e % 2 else (outer, inner)
             uq[e, s, d, pl.ds(n, 1)] = sweep(W[s], cs, low, mid, high)
 
     for k in (6, 7):
-        arrive(k, *DIRECTIONS[k])
+        arrive(k)
     merged = [jnp.where(slot_left, packs_own[0, v], packs_own[1, v]) for v in range(2)]
     for r in range(8):
         for c in range(3):
@@ -249,7 +286,7 @@
         coefficients(r)
 
     for k in (2, 3, 0):
-        arrive(k, *DIRECTIONS[k])
+        arrive(k)
     merged = jnp.where(slot_left, packs_low[0], packs_low[1])
     for r in range(-4, 0):
         for c in range(3):
@@ -258,12 +295,10 @@
     for r in range(-3, 1):
         coefficients(r)
     for k in (4, 5, 1):
-        arrive(k, *DIRECTIONS[k])
+        arrive(k)
     merged = jnp.where(slot_left, packs_high[0], packs_high[1])
-    for r in range(8, 13):
-        for c in range(3):
-            if r < 12 or c == 0:
-                assemble(c, r, merged)
+    for c, r in DOWN:
+        assemble(c, r + 8, merged)
     for r in range(7, 12):
         coefficients(r)
 
@@ -274,10 +309,16 @@
             for n in range(s + 1):
                 edge_row(e, s, n)
 
-    sums = []
-    flag_up = (i < n_gx - 1).astype(F32)
-    flag_low = (i > 0).astype(F32)
+    load_map.wait()
+    layer = lax.broadcasted_iota(jnp.int32, (NZ, LANES), 0)
+    layer_map = jnp.zeros((NZ, LANES), jnp.int32)
+    for z in range(NZ):
+        layer_map = jnp.where(layer == z, map_own[z], layer_map)
     last = SWEEPS - 1
+    flag_left = (j > 0).astype(F32)
+    flag_right = (j < n_gy - 1).astype(F32)
+    pick = (lax.broadcasted_iota(jnp.int32, (LANES, LANES), 0) // BXY == lane_of((LANES, LANES))).astype(F32)
+    extents = (24, 144, 8)
 
     def drop(d, here, above):
         if d == 0:
@@ -286,51 +327,52 @@
             return here - jnp.where(left_end, 0.0, y_next(here)) - 1.0
         return here - jnp.where(top, 0.0, z_next(here)) - 1.0
 
-    energies, squares = [], []
-    for d in range(3):
-        def terms(r, here, above, at_end=False):
-            fall = drop(d, here, above)
-            square = fall * fall
-            t = kp[0, pl.ds(r + 4, 1)] if at_end else face[d, pl.ds(r, 1)]
-            return jnp.concatenate([t * square, square], axis=0)
-
-        main = [terms(r, q_at(last, d, r), q_at(last, d, r + 1) if d == 0 else None) for r in range(8)]
-        up = [terms(r, e_at(0, last, d, r), e_at(0, last, d, r + 1)) for r in range(4)]
-        low = [
-            terms(r, e_at(1, last, d, 7 - r), zero if r == 7 else e_at(1, last, d, 6 - r), d == 0 and r == 7)
-            for r in range(4, 8)
-        ]
-        third = terms(3, e_at(1, last, d, 4), e_at(1, last, d, 3)) if d == 0 else main[3]
-        main_low = main[0] + main[1] + main[2]
-        main_high = main[4] + main[5] + main[6] + main[7]
-        total = main_low + main[3] + main_high
-        total = total + flag_up * (up[0] + up[1] + up[2] + up[3] + main_high)
-        total = total + flag_low * (main_low + third + low[0] + low[1] + low[2] + low[3])
-        own, other = total[:, :, 0:LANES], total[:, :, LANES : 2 * LANES]
-        lane3 = lane_of(own.shape)
-        flag_left = (j > 0).astype(F32)
-        flag_right = (j < n_gy - 1).astype(F32)
-        left = pltpu.roll(other, LANES - LEFT_AT - 4, axis=2) * flag_left
-        right = pltpu.roll(other, LANES - RIGHT_AT - 8, axis=2) * flag_right
-        own = own + jnp.where(lane3 < 8, left, 0.0) + jnp.where(lane3 >= LANES - 8, right, 0.0)
-        sums.append(own)
-    stack = jnp.concatenate(sums, axis=0).reshape(6 * NZ, LANES)
-    pick = (lax.broadcasted_iota(jnp.int32, (LANES, LANES), 0) // BXY == lane_of((LANES, LANES))).astype(F32)
-    blocks = jnp.dot(stack, pick, precision=lax.Precision.HIGHEST, preferred_element_type=F32)
-    blocks = blocks.reshape(3, 2, NZ, LANES)
-
-    load_map.wait()
-    layer = lax.broadcasted_iota(jnp.int32, (NZ, LANES), 0)
-    layer_map = jnp.zeros((NZ, LANES), jnp.int32)
-    for z in range(NZ):
-        layer_map = jnp.where(layer == z, map_own[z], layer_map)
-    extents = (24, 144, 8)
-    perm = [[None] * NCL for _ in range(3)]
-    for n in range(NCL):
-        for d in range(3):
-            held = jnp.where(layer_map == n, blocks[d], 0.0)
-            both = jnp.sum(held, axis=1, keepdims=True)
-            perm[d][n] = both[0] / (both[1] + EPS * extents[d] * extents[d])
+    def coarse(first, along, flag_up, flag_low):
+        e_low, e_high = ENDS.index(first), ENDS.index(first + 7)
+        sums = []
+        for d in along:
+            def terms(n, here, above, at_end=False):
+                fall = drop(d, here, above)
+                square = fall * fall
+                t = kp[0, pl.ds(first + n + 4, 1)] if at_end else face[d, pl.ds(first + n, 1)]
+                return jnp.concatenate([t * square, square], axis=0)
+
+            def main_at(n):
+                return q_at(last, d, first + n)
+
+            main = [terms(n, main_at(n), main_at(n + 1) if d == 0 else None) for n in range(8)]
+            up = [terms(n, e_at(e_low, last, d, n), e_at(e_low, last, d, n + 1)) for n in range(4)]
+            low = [
+                terms(
+                    n, e_at(e_high, last, d, 7 - n), zero if n == 7 else e_at(e_high, last, d, 6 - n), d == 0 and n == 7
+                )
+                for n in range(4, 8)
+            ]
+            third = terms(3, main_at(3), e_at(e_high, last, d, 3)) if d == 0 else main[3]
+            main_low = main[0] + main[1] + main[2]
+            main_high = main[4] + main[5] + main[6] + main[7]
+            total = main_low + main[3] + main_high
+            total = total + flag_up * (up[0] + up[1] + up[2] + up[3] + main_high)
+            total = total + flag_low * (main_low + third + low[0] + low[1] + low[2] + low[3])
+            own, other = total[:, :, 0:LANES], total[:, :, LANES : 2 * LANES]
+            lane3 = lane_of(own.shape)
+            left = pltpu.roll(other, LANES - LEFT_AT - 4, axis=2) * flag_left
+            right = pltpu.roll(other, LANES - RIGHT_AT - 8, axis=2) * flag_right
+            own = own + jnp.where(lane3 < 8, left, 0.0) + jnp.where(lane3 >= LANES - 8, right, 0.0)
+            sums.append(own)
+        count = len(along)
+        stack = jnp.concatenate(sums, axis=0).reshape(2 * count * NZ, LANES)
+        blocks = jnp.dot(stack, pick, precision=lax.Precision.HIGHEST, preferred_element_type=F32)
+        blocks = blocks.reshape(count, 2, NZ, LANES)
+        perm = [[None] * NCL for _ in along]
+        for n in range(NCL):
+            for at, d in enumerate(along):
+                held = jnp.where(layer_map == n, blocks[at], 0.0)
+                both = jnp.sum(held, axis=1, keepdims=True)
+                perm[at][n] = both[0] / (both[1] + EPS * extents[d] * extents[d])
+        return perm
+
+    perm = coarse(0, range(3), (i < n_gx - 1).astype(F32), (i > 0).astype(F32))
     mess[...] = jnp.concatenate(perm[0] + perm[1], axis=0)
 
     def tell(k, di, dj, target):
@@ -339,33 +381,55 @@
             device_id=device(di, dj), device_id_type=MESH,
         )
 
-    last_copies = [(8, -1, 0, mess_x), (9, 0, -1, mess_y)]
-    for k, di, dj, target in last_copies:
-        pl.when(inside(di, dj))(tell(k, di, dj, target).start)
+    first_k = len(copies)
+    last_copies = [
+        (tell(first_k, -1, 0, mess_x), inside(-1, 0) & jnp.logical_not(reaches(-1, 0)), inside(1, 0)),
+        (tell(first_k + 1, 0, -1, mess_y), inside(0, -1), inside(0, 1)),
+    ]
+    for copy, sends, _ in last_copies:
+        pl.when(sends)(copy.start)
+    copies.extend(last_copies)
     for d in range(3):
         for n in range(NCL):
             perm_ref[d, n] = perm[d][n][:, 0 : LANES // BXY]
     for n in range(NCL):
         value = harmonic(perm[2][n], perm[2][n + 1]) if n < NCL - 1 else jnp.zeros((1, LANES), F32)
         trans_ref[2, n] = value[:, 0 : LANES // BXY]
-    for k, (di, dj) in enumerate(DIRECTIONS):
-        pl.when(inside(di, dj))(copies[k].wait_send)
-    for k, di, dj, target in last_copies:
-        copy, here = tell(k, di, dj, target), inside(-di, -dj)
-        pl.when(here)(copy.wait_recv)
-
-        @pl.when(jnp.logical_not(here))
-        def _():
-            target[...] = jnp.zeros(target.shape, F32)
-
+
+    @pl.when(reaches(0, 0))
+    def _():
+        for k in range(8, 14):
+            arrive(k)
+        merged = jnp.where(slot_left, packs_more[0], packs_more[1])
+        for c, r in PLANES[len(DOWN) :]:
+            assemble(c, r + 8, merged)
+        merged = jnp.where(slot_left, packs_far[0], packs_far[1])
+        for c, r in DOWN:
+            assemble(c, r + 16, merged)
+        for r in [8] + list(range(12, 20)):
+            coefficients(r)
+        for s in range(1, SWEEPS):
+            for r in range(12 - s, 20 - s):
+                main_row(s, r, (0,))
+            for e in (2, 3):
+                for n in range(s + 1):
+                    edge_row(e, s, n, (0,))
+        (beyond,) = coarse(8, (0,), (i + 2 < n_gx).astype(F32), 1.0)
+        mess_x[pl.ds(0, NCL)] = jnp.concatenate(beyond, axis=0)
+
+    @pl.when(jnp.logical_not(reaches(0, 0)))
+    def _():
+        arrive(first_k)
+
+    arrive(first_k + 1)
     lane1 = lane_of((1, LANES))
     for n in range(NCL):
         trans_ref[0, n] = harmonic(perm[0][n], mess_x[pl.ds(n, 1)])[:, 0 : LANES // BXY]
         beyond = pltpu.roll(mess_y[pl.ds(NCL + n, 1)], LANES // BXY - 1, axis=1)
         after = jnp.where(lane1 == LANES // BXY - 1, beyond, pltpu.roll(perm[1][n], LANES - 1, axis=1))
         trans_ref[1, n] = harmonic(perm[1][n], after)[:, 0 : LANES // BXY]
-    for k, di, dj, target in last_copies:
-        pl.when(inside(di, dj))(tell(k, di, dj, target).wait_send)
+    for copy, sends, _ in copies:
+        pl.when(sends)(copy.wait_send)
 
 
 def solution(mesh):
@@ -379,7 +443,7 @@
         return pl.pallas_call(
             lambda *refs: kernel(n_gx, n_gy, *refs),
             out_shape=(out, out),
-            in_specs=[pl.BlockSpec(memory_space=pl.ANY)] * 2,
+            in_specs=[pl.BlockSpec(memory_space=pltpu.HBM)] * 2,
             out_specs=(pl.BlockSpec(memory_space=pltpu.VMEM),) * 2,
             scratch_shapes=[
                 vmem(3 * NZ * BXY, LANES),
@@ -391,23 +455,29 @@
                 vmem(2, 2, NZ, LANES),
                 vmem(2, NZ, LANES),
                 vmem(2, NZ, LANES),
+                vmem(len(PLANES) - len(DOWN), NZ, LANES),
+                vmem(len(DOWN), NZ, LANES),
+                vmem(2, NZ, LANES),
+                vmem(2, NZ, LANES),
+                vmem(3, 25, NZ, both),
+                vmem(9, 23, NZ, both),
+                vmem(3, 16, NZ, both),
+                vmem(3, 23, NZ, both),
+                vmem(3, 21, NZ, both),
+                vmem(3, 19, NZ, both),
                 vmem(3, 17, NZ, both),
-                vmem(9, 15, NZ, both),
-                vmem(3, 8, NZ, both),
-                vmem(3, 15, NZ, both),
-                vmem(3, 13, NZ, both),
-                vmem(3, 11, NZ, both),
-                vmem(3, 9, NZ, both),
-                vmem(2, 9, NZ, both),
-                vmem(2, SWEEPS, 3, SWEEPS, NZ, both),
+                vmem(4, 9, NZ, both),
+                vmem(4, SWEEPS, 3, SWEEPS, NZ, both),
                 vmem(NZ, LANES),
                 vmem(NZ, LANES),
                 vmem(NZ, LANES),
                 pltpu.SemaphoreType.DMA((2,)),
-                pltpu.SemaphoreType.DMA((10,)),
-                pltpu.SemaphoreType.DMA((10,)),
+                pltpu.SemaphoreType.DMA((16,)),
+                pltpu.SemaphoreType.DMA((16,)),
             ],
-            compiler_params=pltpu.CompilerParams(collective_id=0, has_side_effects=True),
+            compiler_params=pltpu.CompilerParams(
+                collective_id=0, has_side_effects=True, vmem_limit_bytes=63000000
+            ),
             name="upscale",
         )(k, layer_map)
 

time: 36.5 us -> 35.3 us (0.967)
  the two profiles are of different devices: /device:TPU:1 before, /device:TPU:187 now
where the time goes in v2:
time: 35.3 us; the launch traced here: 35.1 us
  Pallas kernels  32.6 us (92%)
  local copies, waits for them, and re-layouts  1.89 us (5%)
  between operations  0.65 us (2%)
    pallas_call x1, Pallas kernels, local(): pl.pallas_call(lambda *refs: kernel(n_gx, n_gy, *refs), out_shape=(out, o...  32.6 us
    unnamed x4, local copies, waits for them, and re-layouts  1.89 us

profile of v2, /device:TPU:187, one launch (start us, length us, event | category | flops | bytes accessed | tf_op | source)
XLA Modules:
  0.0 35.1 jit_solution(3364418445674220623)
XLA Ops:
  0.6 32.6 %upscale.1 = (f32[3,4,1,16]{3,2,1,0:T(1,128)}, f32[3,4,1,16]{3,2,1,0:T(1,128)}) custom-call(f32[192,128]{1,0:T(8,128)} %bitcast.1, s32[8]{0:T(128)} %refs_1_.1), custom_call_target="tpu_custom_call" | custom-call | tf_op jit(solution)/shard_map/upscale/pallas_call | solution.py:443
  33.2 0.0 copy-start
  33.3 1.3 %copy.6 = f32[3,4,1,16]{3,2,1,0:T(1,128)} copy(f32[3,4,1,16]{3,2,1,0:T(1,128)} %get-tuple-element.4) | data formatting | bytes 1536
  34.6 0.0 copy-done
  34.6 0.6 %copy.7 = f32[3,4,1,16]{3,2,1,0:T(1,128)} copy(f32[3,4,1,16]{3,2,1,0:T(1,128)S(1)} %copy-done) | data formatting | bytes 1536
Async XLA Ops:
  33.2 1.3 %copy-start = (f32[3,4,1,16]{3,2,1,0:T(1,128)S(1)}, f32[3,4,1,16]{3,2,1,0:T(1,128)}, u32[]{:S(2)}) copy-start(f32[3,4,1,16]{3,2,1,0:T(1,128)} %get-tuple-element.5) | copy-start | bytes 2308

commit v3 on v2

--- a/solution.py
+++ b/solution.py
@@ -22,10 +22,16 @@
 PLANES = DOWN + UP[1:] + [(1, 4), (2, 4)]
 PLANE_AT = {cr: at for at, cr in enumerate(PLANES)}
 UP_FROM = PLANE_AT[UP[0]]
-SLOT = 9
-PACKS = [DOWN, UP + [(1, 4), (2, 4)]]
+LAST, FIRST = 4, 13
+PER_PACK = LANES // FIRST
+UP_SET = UP + [(1, 4), (2, 4)]
+PACKS = [DOWN[:PER_PACK], DOWN[PER_PACK:], UP_SET[:PER_PACK], UP_SET[PER_PACK:]]
+UP_SLOT = {cr: (at // PER_PACK, at % PER_PACK * FIRST) for at, cr in enumerate(UP_SET)}
+SLOT_OF = {cr: (2 + v, s) for cr, (v, s) in UP_SLOT.items()}
+SLOT_OF.update({cr: (at // PER_PACK, at % PER_PACK * FIRST) for at, cr in enumerate(DOWN)})
 DIRECTIONS = [(1, 0), (-1, 0), (1, 1), (1, -1), (-1, 1), (-1, -1), (0, 1), (0, -1)]
-MORE = [(-1, 0), (-1, 1), (-1, -1), (-2, 0), (-2, 1), (-2, -1)]
+LOW, HIGH, OWN, FAR = range(4)
+MORE = [(-1, 0), (-1, -1), (-2, 0), (-2, 1), (-2, -1)]
 ENDS = [0, 7, 8, 15]
 LEFT_AT = 20
 RIGHT_AT = 72
@@ -46,9 +52,9 @@
 
 def kernel(
     n_gx, n_gy, k_hbm, map_hbm, perm_ref, trans_ref,
-    k_own, map_own, planes, packs, from_low, from_high, packs_own, packs_low, packs_high,
-    more_high, far_high, packs_more, packs_far,
-    kp, coef, face, q1, q2, q3, q4, u_coef, uq, mess, mess_x, mess_y,
+    k_own, map_own, planes, lasts, packs, from_low, from_high, from_more, from_far,
+    near_lasts, own_packs, low_packs, high_packs, far_packs,
+    kp, coef, face, q1, q2, q3, q4, u_coef, uq, mess, mess_x,
     load_sem, send_sem, recv_sem,
 ):
     i, j = lax.axis_index("gx"), lax.axis_index("gy")
@@ -68,10 +74,9 @@
     def device(di, dj):
         return {"gx": i + di, "gy": j + dj}
 
-    def reaches(di, dj):
-        row, col = i + di, j + dj
-        early = jnp.where(col < n_gy // 2, 1, 3)
-        return (lax.rem(row + 4, 4) == early) & (row + 1 < n_gx)
+    def reaches(di):
+        row = i + di
+        return (lax.rem(row + 4, 4) == 1) & (row + 1 < n_gx)
 
     barrier = pltpu.get_barrier_semaphore()
     for di, dj in DIRECTIONS:
@@ -80,67 +85,69 @@
             pl.semaphore_signal(barrier, inc=1, device_id=device(di, dj), device_id_type=MESH)
 
     signals = 0
-    for di, dj in MORE[3:]:
-        @pl.when(inside(-di, -dj) & reaches(0, 0))
+    for di, dj in MORE[2:]:
+        @pl.when(inside(-di, -dj) & reaches(0))
         def _():
             pl.semaphore_signal(barrier, inc=1, device_id=device(-di, -dj), device_id_type=MESH)
 
-        signals = signals + (inside(di, dj) & reaches(di, dj)).astype(jnp.int32)
+        signals = signals + (inside(di, dj) & reaches(di)).astype(jnp.int32)
 
     lane = lane_of((NZ, LANES))
     load_k.wait()
-    packed = [jnp.zeros((NZ, LANES), F32), jnp.zeros((NZ, LANES), F32)]
+    packed = [jnp.zeros((NZ, LANES), F32)] * len(PACKS)
+    last_of = jnp.zeros((NZ, LANES), F32)
     for at, (c, r) in enumerate(PLANES):
         plane = k_own[pl.ds(c * 64 + r, NZ, stride=8), :]
         planes[at] = plane
+        last_of = jnp.where(between(lane, LAST * at, LAST * at + LAST), pltpu.roll(plane, LAST * at + LAST, axis=1), last_of)
         for v, pack in enumerate(PACKS):
             if (c, r) in pack:
-                s = SLOT * pack.index((c, r))
-                packed[v] = jnp.where(between(lane, s, s + SLOT), pltpu.roll(plane, s + 4, axis=1), packed[v])
-    packs[0] = packed[0]
-    packs[1] = packed[1]
+                s = FIRST * pack.index((c, r))
+                first_of = pltpu.roll(plane, s, axis=1) if s else plane
+                packed[v] = jnp.where(between(lane, s, s + FIRST), first_of, packed[v])
+    lasts[...] = last_of
+    for v, value in enumerate(packed):
+        packs[v] = value
 
     rows_near = 1 + (i > 0).astype(jnp.int32) + (i < n_gx - 1).astype(jnp.int32)
     cols_near = 1 + (j > 0).astype(jnp.int32) + (j < n_gy - 1).astype(jnp.int32)
     pl.semaphore_wait(barrier, rows_near * cols_near - 1 + signals)
 
-    def copy_of(k, di, dj):
-        side = 0 if dj > 0 else 1
-        if dj == 0:
-            if di > 0:
-                source, target = planes.at[pl.ds(UP_FROM, len(UP))], from_low
-            else:
-                source, target = planes.at[pl.ds(0, len(DOWN))], from_high
-        elif di == 0:
-            source, target = packs, packs_own.at[side]
-        elif di > 0:
-            source, target = packs.at[1], packs_low.at[side]
-        else:
-            source, target = packs.at[0], packs_high.at[side]
+    low_half, high_half = pl.ds(0, 2), pl.ds(2, 2)
+
+    def remote(k, source, target, di, dj):
         return pltpu.make_async_remote_copy(
             src_ref=source, dst_ref=target, send_sem=send_sem.at[k], recv_sem=recv_sem.at[k],
             device_id=device(di, dj), device_id_type=MESH,
         )
 
+    def copy_of(k, di, dj):
+        if dj == 0:
+            if di > 0:
+                return remote(k, planes.at[pl.ds(UP_FROM, len(UP))], from_low, di, dj)
+            return remote(k, planes.at[pl.ds(0, len(DOWN))], from_high, di, dj)
+        if dj > 0:
+            return remote(k, lasts, near_lasts.at[LOW if di > 0 else HIGH if di < 0 else OWN], di, dj)
+        if di == 0:
+            return remote(k, packs, own_packs, di, dj)
+        if di > 0:
+            return remote(k, packs.at[high_half], low_packs, di, dj)
+        return remote(k, packs.at[low_half], high_packs.at[low_half], di, dj)
+
     def more_of(k, di, dj):
-        side = 0 if dj > 0 else 1
+        if di == -1:
+            if dj == 0:
+                return remote(k, planes.at[pl.ds(len(DOWN), len(PLANES) - len(DOWN))], from_more, di, dj)
+            return remote(k, packs.at[high_half], high_packs.at[high_half], di, dj)
         if dj == 0:
-            if di == -1:
-                source, target = planes.at[pl.ds(len(DOWN), len(PLANES) - len(DOWN))], more_high
-            else:
-                source, target = planes.at[pl.ds(0, len(DOWN))], far_high
-        elif di == -1:
-            source, target = packs.at[1], packs_more.at[side]
-        else:
-            source, target = packs.at[0], packs_far.at[side]
-        return pltpu.make_async_remote_copy(
-            src_ref=source, dst_ref=target, send_sem=send_sem.at[k], recv_sem=recv_sem.at[k],
-            device_id=device(di, dj), device_id_type=MESH,
-        )
+            return remote(k, planes.at[pl.ds(0, len(DOWN))], from_far, di, dj)
+        if dj > 0:
+            return remote(k, lasts, near_lasts.at[FAR], di, dj)
+        return remote(k, packs.at[low_half], far_packs, di, dj)
 
     copies = [(copy_of(k, *to), inside(*to), inside(-to[0], -to[1])) for k, to in enumerate(DIRECTIONS)]
     for k, (di, dj) in enumerate(MORE):
-        sends = inside(di, dj) & reaches(di, dj)
+        sends = inside(di, dj) & reaches(di)
         copies.append((more_of(len(DIRECTIONS) + k, di, dj), sends, inside(-di, -dj)))
     for copy, sends, _ in copies:
         pl.when(sends)(copy.start)
@@ -154,36 +161,36 @@
         def _():
             target[...] = jnp.zeros(target.shape, F32)
 
-    edge = (lane >= LANES - 4) | (lane < 5)
-    slot_left = lax.rem(lane, SLOT) < 4
-
-    def assemble(c, r, merged):
+    edge = (lane >= LANES - LAST) | (lane < FIRST)
+
+    def assemble(c, r):
         if 0 <= r < 8:
-            own = planes[PLANE_AT[c, r]]
-            v = 0 if (c, r) in DOWN else 1
-            s = SLOT * PACKS[v].index((c, r))
-            pack = merged[v]
+            at, v, s = PLANE_AT[c, r], *SLOT_OF[c, r]
+            own, side, firsts = planes[at], OWN, own_packs[v]
         elif r < 0:
-            at = UP.index((c, r + 8))
-            own, s, pack = from_low[at], SLOT * at, merged
-        elif r >= 16 or (c, r - 8) in DOWN:
-            at = DOWN.index((c, r % 8))
-            own, s, pack = (from_high if r < 16 else far_high)[at], SLOT * at, merged
+            at, v, s = PLANE_AT[c, r + 8], *UP_SLOT[c, r + 8]
+            own, side, firsts = from_low[at - UP_FROM], LOW, low_packs[v]
+        elif r >= 16:
+            at, v, s = PLANE_AT[c, r - 16], *SLOT_OF[c, r - 16]
+            own, side, firsts = from_far[at], FAR, far_packs[v]
         else:
-            at = PLANE_AT[c, r - 8] - len(DOWN)
-            own, s, pack = more_high[at], SLOT * PACKS[1].index((c, r - 8)), merged
-        margin = pltpu.roll(pack, (2 * LANES - s - 4) % LANES, axis=1)
-        left = pltpu.roll(jnp.where(lane >= LANES - 4, margin, own), LEFT_AT + 4, axis=1)
-        right = pltpu.roll(jnp.where(lane < 5, margin, own), RIGHT_AT + 8, axis=1)
+            at, v, s = PLANE_AT[c, r - 8], *SLOT_OF[c, r - 8]
+            own = from_high[at] if at < len(DOWN) else from_more[at - len(DOWN)]
+            side, firsts = HIGH, high_packs[v]
+        before = pltpu.roll(near_lasts[side], LANES - LAST - LAST * at, axis=1)
+        after = pltpu.roll(firsts, LANES - s, axis=1) if s else firsts
+        margin = jnp.where(lane < FIRST, after, before)
+        left = pltpu.roll(jnp.where(lane >= LANES - LAST, margin, own), LEFT_AT + 4, axis=1)
+        right = pltpu.roll(jnp.where(lane < BXY, margin, own), RIGHT_AT + 8, axis=1)
         other = jnp.where(between(lane, LEFT_AT, LEFT_AT + 12), left, 1.0)
-        other = jnp.where(between(lane, RIGHT_AT, RIGHT_AT + 13), right, other)
+        other = jnp.where(between(lane, RIGHT_AT, RIGHT_AT + 16), right, other)
         other = jnp.where(edge, margin, other)
         kp[c, r + 4, :, 0:LANES] = own + KMIN
         kp[c, r + 4, :, LANES : 2 * LANES] = other + KMIN
 
     lane2 = lane_of((1, NZ, 2 * LANES))
     layer2 = lax.broadcasted_iota(jnp.int32, (1, NZ, 2 * LANES), 1)
-    left_end = lane2 == LANES + LEFT_AT + 11
+    left_end = (lane2 == LANES + LEFT_AT + 11) | (lane2 == LANES + RIGHT_AT + 15)
     right_start = lane2 == LANES + RIGHT_AT
     top, bottom = layer2 == NZ - 1, layer2 == 0
     zero = jnp.zeros((1, NZ, 2 * LANES), F32)
@@ -278,27 +285,22 @@
 
     for k in (6, 7):
         arrive(k)
-    merged = [jnp.where(slot_left, packs_own[0, v], packs_own[1, v]) for v in range(2)]
     for r in range(8):
         for c in range(3):
-            assemble(c, r, merged)
+            assemble(c, r)
     for r in range(1, 7):
         coefficients(r)
 
     for k in (2, 3, 0):
         arrive(k)
-    merged = jnp.where(slot_left, packs_low[0], packs_low[1])
-    for r in range(-4, 0):
-        for c in range(3):
-            if r > -4 or c == 0:
-                assemble(c, r, merged)
+    for c, r in UP:
+        assemble(c, r - 8)
     for r in range(-3, 1):
         coefficients(r)
     for k in (4, 5, 1):
         arrive(k)
-    merged = jnp.where(slot_left, packs_high[0], packs_high[1])
     for c, r in DOWN:
-        assemble(c, r + 8, merged)
+        assemble(c, r + 8)
     for r in range(7, 12):
         coefficients(r)
 
@@ -360,6 +362,11 @@
             right = pltpu.roll(other, LANES - RIGHT_AT - 8, axis=2) * flag_right
             own = own + jnp.where(lane3 < 8, left, 0.0) + jnp.where(lane3 >= LANES - 8, right, 0.0)
             sums.append(own)
+            if d == 1:
+                after = other + pltpu.roll(other, LANES - RIGHT_AT - 8, axis=2)
+        if len(along) == 3:
+            sums.append(after)
+            along = [*along, 1]
         count = len(along)
         stack = jnp.concatenate(sums, axis=0).reshape(2 * count * NZ, LANES)
         blocks = jnp.dot(stack, pick, precision=lax.Precision.HIGHEST, preferred_element_type=F32)
@@ -373,22 +380,13 @@
         return perm
 
     perm = coarse(0, range(3), (i < n_gx - 1).astype(F32), (i > 0).astype(F32))
-    mess[...] = jnp.concatenate(perm[0] + perm[1], axis=0)
-
-    def tell(k, di, dj, target):
-        return pltpu.make_async_remote_copy(
-            src_ref=mess, dst_ref=target, send_sem=send_sem.at[k], recv_sem=recv_sem.at[k],
-            device_id=device(di, dj), device_id_type=MESH,
-        )
-
-    first_k = len(copies)
-    last_copies = [
-        (tell(first_k, -1, 0, mess_x), inside(-1, 0) & jnp.logical_not(reaches(-1, 0)), inside(1, 0)),
-        (tell(first_k + 1, 0, -1, mess_y), inside(0, -1), inside(0, 1)),
-    ]
-    for copy, sends, _ in last_copies:
-        pl.when(sends)(copy.start)
-    copies.extend(last_copies)
+    mess[pl.ds(0, NCL)] = jnp.concatenate(perm[0], axis=0)
+
+    tell_k = len(copies)
+    tell = remote(tell_k, mess, mess_x, -1, 0)
+    sends = inside(-1, 0) & jnp.logical_not(reaches(-1))
+    pl.when(sends)(tell.start)
+    copies.append((tell, sends, inside(1, 0)))
     for d in range(3):
         for n in range(NCL):
             perm_ref[d, n] = perm[d][n][:, 0 : LANES // BXY]
@@ -396,16 +394,21 @@
         value = harmonic(perm[2][n], perm[2][n + 1]) if n < NCL - 1 else jnp.zeros((1, LANES), F32)
         trans_ref[2, n] = value[:, 0 : LANES // BXY]
 
-    @pl.when(reaches(0, 0))
+    exists = (j < n_gy - 1).astype(F32)
+    lane1 = lane_of((1, LANES))
+    for n in range(NCL):
+        beyond = pltpu.roll(perm[3][n], LANES // BXY - 1, axis=1) * exists
+        after = jnp.where(lane1 == LANES // BXY - 1, beyond, pltpu.roll(perm[1][n], LANES - 1, axis=1))
+        trans_ref[1, n] = harmonic(perm[1][n], after)[:, 0 : LANES // BXY]
+
+    @pl.when(reaches(0))
     def _():
-        for k in range(8, 14):
+        for k in range(8, 13):
             arrive(k)
-        merged = jnp.where(slot_left, packs_more[0], packs_more[1])
         for c, r in PLANES[len(DOWN) :]:
-            assemble(c, r + 8, merged)
-        merged = jnp.where(slot_left, packs_far[0], packs_far[1])
+            assemble(c, r + 8)
         for c, r in DOWN:
-            assemble(c, r + 16, merged)
+            assemble(c, r + 16)
         for r in [8] + list(range(12, 20)):
             coefficients(r)
         for s in range(1, SWEEPS):
@@ -417,17 +420,12 @@
         (beyond,) = coarse(8, (0,), (i + 2 < n_gx).astype(F32), 1.0)
         mess_x[pl.ds(0, NCL)] = jnp.concatenate(beyond, axis=0)
 
-    @pl.when(jnp.logical_not(reaches(0, 0)))
+    @pl.when(jnp.logical_not(reaches(0)))
     def _():
-        arrive(first_k)
-
-    arrive(first_k + 1)
-    lane1 = lane_of((1, LANES))
+        arrive(tell_k)
+
     for n in range(NCL):
         trans_ref[0, n] = harmonic(perm[0][n], mess_x[pl.ds(n, 1)])[:, 0 : LANES // BXY]
-        beyond = pltpu.roll(mess_y[pl.ds(NCL + n, 1)], LANES // BXY - 1, axis=1)
-        after = jnp.where(lane1 == LANES // BXY - 1, beyond, pltpu.roll(perm[1][n], LANES - 1, axis=1))
-        trans_ref[1, n] = harmonic(perm[1][n], after)[:, 0 : LANES // BXY]
     for copy, sends, _ in copies:
         pl.when(sends)(copy.wait_send)
 
@@ -449,15 +447,16 @@
                 vmem(3 * NZ * BXY, LANES),
                 pltpu.SMEM((NZ,), jnp.int32),
                 vmem(len(PLANES), NZ, LANES),
-                vmem(2, NZ, LANES),
+                vmem(NZ, LANES),
+                vmem(4, NZ, LANES),
                 vmem(len(UP), NZ, LANES),
                 vmem(len(DOWN), NZ, LANES),
-                vmem(2, 2, NZ, LANES),
-                vmem(2, NZ, LANES),
-                vmem(2, NZ, LANES),
                 vmem(len(PLANES) - len(DOWN), NZ, LANES),
                 vmem(len(DOWN), NZ, LANES),
+                vmem(4, NZ, LANES),
+                vmem(4, NZ, LANES),
                 vmem(2, NZ, LANES),
+                vmem(4, NZ, LANES),
                 vmem(2, NZ, LANES),
                 vmem(3, 25, NZ, both),
                 vmem(9, 23, NZ, both),
@@ -470,13 +469,12 @@
                 vmem(4, SWEEPS, 3, SWEEPS, NZ, both),
                 vmem(NZ, LANES),
                 vmem(NZ, LANES),
-                vmem(NZ, LANES),
                 pltpu.SemaphoreType.DMA((2,)),
-                pltpu.SemaphoreType.DMA((16,)),
-                pltpu.SemaphoreType.DMA((16,)),
+                pltpu.SemaphoreType.DMA((14,)),
+                pltpu.SemaphoreType.DMA((14,)),
             ],
             compiler_params=pltpu.CompilerParams(
-                collective_id=0, has_side_effects=True, vmem_limit_bytes=63000000
+                collective_id=0, has_side_effects=True, vmem_limit_bytes=56440000
             ),
             name="upscale",
         )(k, layer_map)

time: 35.3 us -> 35 us (level)
  the two profiles are of different devices: /device:TPU:187 before, /device:TPU:463 now
where the time goes in v3:
time: 35 us; the launch traced here: 34.9 us
  Pallas kernels  32.4 us (93%)
  local copies, waits for them, and re-layouts  1.84 us (5%)
  between operations  0.65 us (2%)
    pallas_call x1, Pallas kernels, local(): pl.pallas_call(lambda *refs: kernel(n_gx, n_gy, *refs), out_shape=(out, o...  32.4 us
    unnamed x4, local copies, waits for them, and re-layouts  1.84 us

profile of v3, /device:TPU:463, one launch (start us, length us, event | category | flops | bytes accessed | tf_op | source)
XLA Modules:
  0.0 34.9 jit_solution(8799441032264412886)
XLA Ops:
  0.6 0.0 copy-start
  0.6 0.6 %copy-done = s32[8]{0:T(128)S(1)} copy-done((s32[8]{0:T(128)S(1)}, s32[8]{0:T(128)}, u32[]{:S(2)}) %copy-start) | copy-done | bytes 56
  1.3 32.4 %upscale.1 = (f32[3,4,1,16]{3,2,1,0:T(1,128)S(1)}, f32[3,4,1,16]{3,2,1,0:T(1,128)S(1)}) custom-call(f32[192,128]{1,0:T(8,128)} %bitcast.1, s32[8]{0:T(128)S(1)} %copy-done), custom_call_target="tpu_custom_call" | custom-call | tf_op jit(solution)/shard_map/upscale/pallas_call | solution.py:441
  33.7 0.6 %copy.6 = f32[3,4,1,16]{3,2,1,0:T(1,128)} copy(f32[3,4,1,16]{3,2,1,0:T(1,128)S(1)} %get-tuple-element.4) | data formatting | bytes 1536
  34.3 0.6 %copy.7 = f32[3,4,1,16]{3,2,1,0:T(1,128)} copy(f32[3,4,1,16]{3,2,1,0:T(1,128)S(1)} %get-tuple-element.5) | data formatting | bytes 1536
Async XLA Ops:
  0.6 0.7 %copy-start = (s32[8]{0:T(128)S(1)}, s32[8]{0:T(128)}, u32[]{:S(2)}) copy-start(s32[8]{0:T(128)} %refs_1_.1) | copy-start | bytes 100

commit v4 on v3

--- a/solution.py
+++ b/solution.py
@@ -76,7 +76,7 @@
 
     def reaches(di):
         row = i + di
-        return (lax.rem(row + 4, 4) == 1) & (row + 1 < n_gx)
+        return (lax.rem(row + 2, 2) == 1) & (row + 1 < n_gx)
 
     barrier = pltpu.get_barrier_semaphore()
     for di, dj in DIRECTIONS:
@@ -474,10 +474,10 @@
                 pltpu.SemaphoreType.DMA((14,)),
             ],
             compiler_params=pltpu.CompilerParams(
-                collective_id=0, has_side_effects=True, vmem_limit_bytes=56440000
+                collective_id=0, has_side_effects=True, vmem_limit_bytes=32 * 1024 * 1024
             ),
             name="upscale",
-        )(k, layer_map)
+        )(pltpu.with_memory_space_constraint(k, pltpu.HBM), pltpu.with_memory_space_constraint(layer_map, pltpu.HBM))
 
     spec = P(None, None, "gx", "gy")
     return jax.shard_map(local, mesh=mesh, in_specs=(spec, P()), out_specs=(spec, spec), check_vma=False)

time: 35 us -> 31.5 us (0.900)
  the two profiles are of different devices: /device:TPU:463 before, /device:TPU:41 now
where the time goes in v4:
time: 31.5 us; the launch traced here: 31.3 us
  Pallas kernels  29.5 us (94%)
  local copies, waits for them, and re-layouts  1.19 us (4%)
  between operations  0.64 us (2%)
    pallas_call x1, Pallas kernels, local(): pl.pallas_call(lambda *refs: kernel(n_gx, n_gy, *refs), out_shape=(out, o...  29.5 us
    unnamed x2, local copies, waits for them, and re-layouts  1.19 us

profile of v4, /device:TPU:41, one launch (start us, length us, event | category | flops | bytes accessed | tf_op | source)
XLA Modules:
  0.0 31.3 jit_solution(5869251580794558138)
XLA Ops:
  0.6 29.5 %upscale.1 = (f32[3,4,1,16]{3,2,1,0:T(1,128)S(1)}, f32[3,4,1,16]{3,2,1,0:T(1,128)S(1)}) custom-call(f32[192,128]{1,0:T(8,128)} %bitcast.1, s32[8]{0:T(128)} %refs_1_.1), custom_call_target="tpu_custom_call" | custom-call | tf_op jit(solution)/shard_map/upscale/pallas_call | solution.py:441
  30.1 0.6 %copy.6 = f32[3,4,1,16]{3,2,1,0:T(1,128)} copy(f32[3,4,1,16]{3,2,1,0:T(1,128)S(1)} %get-tuple-element.4) | data formatting | bytes 1536
  30.7 0.6 %copy.7 = f32[3,4,1,16]{3,2,1,0:T(1,128)} copy(f32[3,4,1,16]{3,2,1,0:T(1,128)S(1)} %get-tuple-element.5) | data formatting | bytes 1536

commit v5 on v4

--- a/solution.py
+++ b/solution.py
@@ -24,15 +24,26 @@
 UP_FROM = PLANE_AT[UP[0]]
 LAST, FIRST = 4, 13
 PER_PACK = LANES // FIRST
-UP_SET = UP + [(1, 4), (2, 4)]
-PACKS = [DOWN[:PER_PACK], DOWN[PER_PACK:], UP_SET[:PER_PACK], UP_SET[PER_PACK:]]
-UP_SLOT = {cr: (at // PER_PACK, at % PER_PACK * FIRST) for at, cr in enumerate(UP_SET)}
-SLOT_OF = {cr: (2 + v, s) for cr, (v, s) in UP_SLOT.items()}
-SLOT_OF.update({cr: (at // PER_PACK, at % PER_PACK * FIRST) for at, cr in enumerate(DOWN)})
+LISTS = [DOWN, UP + [(1, 4), (2, 4)]]
+PACKS = [part for planes in LISTS for part in (planes[:PER_PACK], planes[PER_PACK:])]
+SLOT_OF = {cr: (v, FIRST * at) for v, pack in reversed(list(enumerate(PACKS))) for at, cr in enumerate(pack)}
+
+
+def slots(widths):
+    at, result = 0, {}
+    for cr, width in widths.items():
+        result[cr] = (at, width)
+        at = at + width
+    assert at <= LANES
+    return result
+
+
+UP_SLOTS = slots({cr: 12 for cr in UP})
+DOWN_WIDTHS = {0: [11, 11, 10, 9, 3], 1: [12, 11, 10, 4], 2: [11, 10, 9, 3]}
+DOWN_SLOTS = slots({(c, r): DOWN_WIDTHS[c][r] for c, r in DOWN})
 DIRECTIONS = [(1, 0), (-1, 0), (1, 1), (1, -1), (-1, 1), (-1, -1), (0, 1), (0, -1)]
-LOW, HIGH, OWN, FAR = range(4)
-MORE = [(-1, 0), (-1, -1), (-2, 0), (-2, 1), (-2, -1)]
-ENDS = [0, 7, 8, 15]
+LOW, HIGH, OWN = range(3)
+ENDS = [0, 7, 8]
 LEFT_AT = 20
 RIGHT_AT = 72
 W = [1.0 / (1.05 + 0.95 * math.cos(math.pi * (2 * s + 1) / (2 * SWEEPS))) for s in range(SWEEPS)]
@@ -52,8 +63,8 @@
 
 def kernel(
     n_gx, n_gy, k_hbm, map_hbm, perm_ref, trans_ref,
-    k_own, map_own, planes, lasts, packs, from_low, from_high, from_more, from_far,
-    near_lasts, own_packs, low_packs, high_packs, far_packs,
+    k_own, map_own, planes, lasts, packs, corners, from_low, from_high,
+    near_lasts, own_packs, low_pack, high_pack, tale, heard,
     kp, coef, face, q1, q2, q3, q4, u_coef, uq, mess, mess_x,
     load_sem, send_sem, recv_sem,
 ):
@@ -74,9 +85,8 @@
     def device(di, dj):
         return {"gx": i + di, "gy": j + dj}
 
-    def reaches(di):
-        row = i + di
-        return (lax.rem(row + 2, 2) == 1) & (row + 1 < n_gx)
+    odd = lax.rem(i, 2) == 1
+    even = jnp.logical_not(odd)
 
     barrier = pltpu.get_barrier_semaphore()
     for di, dj in DIRECTIONS:
@@ -84,17 +94,10 @@
         def _():
             pl.semaphore_signal(barrier, inc=1, device_id=device(di, dj), device_id_type=MESH)
 
-    signals = 0
-    for di, dj in MORE[2:]:
-        @pl.when(inside(-di, -dj) & reaches(0))
-        def _():
-            pl.semaphore_signal(barrier, inc=1, device_id=device(-di, -dj), device_id_type=MESH)
-
-        signals = signals + (inside(di, dj) & reaches(di)).astype(jnp.int32)
-
     lane = lane_of((NZ, LANES))
     load_k.wait()
     packed = [jnp.zeros((NZ, LANES), F32)] * len(PACKS)
+    corner = [jnp.zeros((NZ, LANES), F32)] * 2
     last_of = jnp.zeros((NZ, LANES), F32)
     for at, (c, r) in enumerate(PLANES):
         plane = k_own[pl.ds(c * 64 + r, NZ, stride=8), :]
@@ -105,15 +108,20 @@
                 s = FIRST * pack.index((c, r))
                 first_of = pltpu.roll(plane, s, axis=1) if s else plane
                 packed[v] = jnp.where(between(lane, s, s + FIRST), first_of, packed[v])
+        for v, places in enumerate((DOWN_SLOTS, UP_SLOTS)):
+            if (c, r) in places:
+                s, width = places[c, r]
+                first_of = pltpu.roll(plane, s, axis=1) if s else plane
+                corner[v] = jnp.where(between(lane, s, s + width), first_of, corner[v])
     lasts[...] = last_of
+    corners[0] = corner[0]
+    corners[1] = corner[1]
     for v, value in enumerate(packed):
         packs[v] = value
 
     rows_near = 1 + (i > 0).astype(jnp.int32) + (i < n_gx - 1).astype(jnp.int32)
     cols_near = 1 + (j > 0).astype(jnp.int32) + (j < n_gy - 1).astype(jnp.int32)
-    pl.semaphore_wait(barrier, rows_near * cols_near - 1 + signals)
-
-    low_half, high_half = pl.ds(0, 2), pl.ds(2, 2)
+    pl.semaphore_wait(barrier, rows_near * cols_near - 1)
 
     def remote(k, source, target, di, dj):
         return pltpu.make_async_remote_copy(
@@ -131,24 +139,10 @@
         if di == 0:
             return remote(k, packs, own_packs, di, dj)
         if di > 0:
-            return remote(k, packs.at[high_half], low_packs, di, dj)
-        return remote(k, packs.at[low_half], high_packs.at[low_half], di, dj)
-
-    def more_of(k, di, dj):
-        if di == -1:
-            if dj == 0:
-                return remote(k, planes.at[pl.ds(len(DOWN), len(PLANES) - len(DOWN))], from_more, di, dj)
-            return remote(k, packs.at[high_half], high_packs.at[high_half], di, dj)
-        if dj == 0:
-            return remote(k, planes.at[pl.ds(0, len(DOWN))], from_far, di, dj)
-        if dj > 0:
-            return remote(k, lasts, near_lasts.at[FAR], di, dj)
-        return remote(k, packs.at[low_half], far_packs, di, dj)
+            return remote(k, corners.at[1], low_pack, di, dj)
+        return remote(k, corners.at[0], high_pack, di, dj)
 
     copies = [(copy_of(k, *to), inside(*to), inside(-to[0], -to[1])) for k, to in enumerate(DIRECTIONS)]
-    for k, (di, dj) in enumerate(MORE):
-        sends = inside(di, dj) & reaches(di)
-        copies.append((more_of(len(DIRECTIONS) + k, di, dj), sends, inside(-di, -dj)))
     for copy, sends, _ in copies:
         pl.when(sends)(copy.start)
 
@@ -165,18 +159,14 @@
 
     def assemble(c, r):
         if 0 <= r < 8:
-            at, v, s = PLANE_AT[c, r], *SLOT_OF[c, r]
+            at, (v, s) = PLANE_AT[c, r], SLOT_OF[c, r]
             own, side, firsts = planes[at], OWN, own_packs[v]
         elif r < 0:
-            at, v, s = PLANE_AT[c, r + 8], *UP_SLOT[c, r + 8]
-            own, side, firsts = from_low[at - UP_FROM], LOW, low_packs[v]
-        elif r >= 16:
-            at, v, s = PLANE_AT[c, r - 16], *SLOT_OF[c, r - 16]
-            own, side, firsts = from_far[at], FAR, far_packs[v]
+            at, s = PLANE_AT[c, r + 8], UP_SLOTS[c, r + 8][0]
+            own, side, firsts = from_low[at - UP_FROM], LOW, low_pack[...]
         else:
-            at, v, s = PLANE_AT[c, r - 8], *SLOT_OF[c, r - 8]
-            own = from_high[at] if at < len(DOWN) else from_more[at - len(DOWN)]
-            side, firsts = HIGH, high_packs[v]
+            at, s = PLANE_AT[c, r - 8], DOWN_SLOTS[c, r - 8][0]
+            own, side, firsts = from_high[at], HIGH, high_pack[...]
         before = pltpu.roll(near_lasts[side], LANES - LAST - LAST * at, axis=1)
         after = pltpu.roll(firsts, LANES - s, axis=1) if s else firsts
         margin = jnp.where(lane < FIRST, after, before)
@@ -235,7 +225,7 @@
             coef[n, pl.ds(r + 3, 1)] = value
             if n >= 6:
                 q1[n - 6, pl.ds(r + 3, 1)] = W[0] * value
-        if 0 <= r < 16:
+        if 0 <= r < 12:
             for d, value in enumerate((tx_high, ty_high, tz_high)):
                 if r < 8 or d == 0:
                     face[d, pl.ds(r, 1)] = value
@@ -261,6 +251,8 @@
     qs = [(q1, 3), (q2, 2), (q3, 1), (q4, 0)]
 
     def q_at(s, d, r):
+        if r == 12:
+            return jnp.concatenate([heard[pl.ds(s, 1)], heard[pl.ds(SWEEPS + 1 + s, 1)]], axis=2)
         ref, offset = qs[s]
         return ref[d, pl.ds(r + offset, 1)]
 
@@ -283,6 +275,51 @@
             low, high = (inner, outer) if e % 2 else (outer, inner)
             uq[e, s, d, pl.ds(n, 1)] = sweep(W[s], cs, low, mid, high)
 
+    last = SWEEPS - 1
+    flag_left = (j > 0).astype(F32)
+    flag_right = (j < n_gy - 1).astype(F32)
+    flag_up = (i < n_gx - 1).astype(F32)
+    flag_low = (i > 0).astype(F32)
+
+    def terms(d, r, here, above, at_end=False):
+        if d == 0:
+            fall = here - above - 1.0
+        elif d == 1:
+            fall = here - jnp.where(left_end, 0.0, y_next(here)) - 1.0
+        else:
+            fall = here - jnp.where(top, 0.0, z_next(here)) - 1.0
+        square = fall * fall
+        t = kp[0, pl.ds(r + 4, 1)] if at_end else face[d, pl.ds(r, 1)]
+        return jnp.concatenate([t * square, square], axis=0)
+
+    def main_terms(d, r):
+        return terms(d, r, q_at(last, d, r), q_at(last, d, r + 1) if d == 0 else None)
+
+    def upper_sums(d):
+        main = [main_terms(d, r) for r in range(4, 8)]
+        main = main[0] + main[1] + main[2] + main[3]
+        ends = [
+            terms(d, r, e_at(1, last, d, 7 - r), zero if r == 7 else e_at(1, last, d, 6 - r), d == 0 and r == 7)
+            for r in range(4, 8)
+        ]
+        return main + flag_up * main + flag_low * (ends[0] + ends[1] + ends[2] + ends[3])
+
+    def lower_sums(d, first, ended, up, low):
+        e = ENDS.index(first)
+        main = [main_terms(d, first + n) for n in range(4)]
+        ends = [terms(d, first + n, e_at(e, last, d, n), e_at(e, last, d, n + 1)) for n in range(4)]
+        third = terms(d, first + 3, q_at(last, d, first + 3), ended) if d == 0 else main[3]
+        three = main[0] + main[1] + main[2]
+        return three + main[3] + up * (ends[0] + ends[1] + ends[2] + ends[3]) + low * (three + third)
+
+    def columns(total):
+        own, other = total[:, :, 0:LANES], total[:, :, LANES : 2 * LANES]
+        lane3 = lane_of(own.shape)
+        left = pltpu.roll(other, LANES - LEFT_AT - 4, axis=2) * flag_left
+        right = pltpu.roll(other, LANES - RIGHT_AT - 8, axis=2)
+        own = own + jnp.where(lane3 < 8, left, 0.0) + jnp.where(lane3 >= LANES - 8, right * flag_right, 0.0)
+        return own, other + right
+
     for k in (6, 7):
         arrive(k)
     for r in range(8):
@@ -291,82 +328,62 @@
     for r in range(1, 7):
         coefficients(r)
 
-    for k in (2, 3, 0):
-        arrive(k)
-    for c, r in UP:
-        assemble(c, r - 8)
-    for r in range(-3, 1):
-        coefficients(r)
-    for k in (4, 5, 1):
-        arrive(k)
-    for c, r in DOWN:
-        assemble(c, r + 8)
-    for r in range(7, 12):
-        coefficients(r)
-
-    for s in range(1, SWEEPS):
-        for r in range(s - 4 + 1, 12 - s):
-            main_row(s, r)
-        for e in range(2):
+    def from_below():
+        for k in (2, 3, 0):
+            arrive(k)
+        for c, r in UP:
+            assemble(c, r - 8)
+        for r in range(-3, 1):
+            coefficients(r)
+
+    def from_above():
+        for k in (4, 5, 1):
+            arrive(k)
+        for c, r in DOWN:
+            assemble(c, r + 8)
+        for r in range(7, 12):
+            coefficients(r)
+
+    def sweeps(starts, stops, e):
+        for s in range(1, SWEEPS):
+            for r in range(starts[s - 1], stops[s - 1]):
+                main_row(s, r, range(3) if r < 12 - s - 1 else (0,))
             for n in range(s + 1):
                 edge_row(e, s, n)
+
+    told = remote(len(copies), tale, heard, -1, 0)
+    tells = even & (i > 0)
+    copies.append((told, tells, odd & (i + 1 < n_gx)))
+
+    @pl.when(even)
+    def _():
+        from_above()
+        sweeps((2, 3, 4), (11, 10, 9), 1)
+        for s in range(SWEEPS + 1):
+            value = q_at(s, 0, 4) if s < SWEEPS else e_at(1, last, 0, 3)
+            tale[pl.ds(s, 1)] = value[:, :, 0:LANES]
+            tale[pl.ds(SWEEPS + 1 + s, 1)] = value[:, :, LANES : 2 * LANES]
+        tale[pl.ds(2 * SWEEPS + 2, 2)] = columns(upper_sums(0))[0]
+        pl.when(tells)(told.start)
+        from_below()
+        sweeps((-2, -1, 0), (2, 3, 4), 0)
+
+    @pl.when(odd)
+    def _():
+        from_below()
+        sweeps((-2, -1, 0), (6, 5, 4), 0)
+        from_above()
+        sweeps((6, 5, 4), (11, 10, 9), 1)
 
     load_map.wait()
     layer = lax.broadcasted_iota(jnp.int32, (NZ, LANES), 0)
     layer_map = jnp.zeros((NZ, LANES), jnp.int32)
     for z in range(NZ):
         layer_map = jnp.where(layer == z, map_own[z], layer_map)
-    last = SWEEPS - 1
-    flag_left = (j > 0).astype(F32)
-    flag_right = (j < n_gy - 1).astype(F32)
     pick = (lax.broadcasted_iota(jnp.int32, (LANES, LANES), 0) // BXY == lane_of((LANES, LANES))).astype(F32)
     extents = (24, 144, 8)
 
-    def drop(d, here, above):
-        if d == 0:
-            return here - above - 1.0
-        if d == 1:
-            return here - jnp.where(left_end, 0.0, y_next(here)) - 1.0
-        return here - jnp.where(top, 0.0, z_next(here)) - 1.0
-
-    def coarse(first, along, flag_up, flag_low):
-        e_low, e_high = ENDS.index(first), ENDS.index(first + 7)
-        sums = []
-        for d in along:
-            def terms(n, here, above, at_end=False):
-                fall = drop(d, here, above)
-                square = fall * fall
-                t = kp[0, pl.ds(first + n + 4, 1)] if at_end else face[d, pl.ds(first + n, 1)]
-                return jnp.concatenate([t * square, square], axis=0)
-
-            def main_at(n):
-                return q_at(last, d, first + n)
-
-            main = [terms(n, main_at(n), main_at(n + 1) if d == 0 else None) for n in range(8)]
-            up = [terms(n, e_at(e_low, last, d, n), e_at(e_low, last, d, n + 1)) for n in range(4)]
-            low = [
-                terms(
-                    n, e_at(e_high, last, d, 7 - n), zero if n == 7 else e_at(e_high, last, d, 6 - n), d == 0 and n == 7
-                )
-                for n in range(4, 8)
-            ]
-            third = terms(3, main_at(3), e_at(e_high, last, d, 3)) if d == 0 else main[3]
-            main_low = main[0] + main[1] + main[2]
-            main_high = main[4] + main[5] + main[6] + main[7]
-            total = main_low + main[3] + main_high
-            total = total + flag_up * (up[0] + up[1] + up[2] + up[3] + main_high)
-            total = total + flag_low * (main_low + third + low[0] + low[1] + low[2] + low[3])
-            own, other = total[:, :, 0:LANES], total[:, :, LANES : 2 * LANES]
-            lane3 = lane_of(own.shape)
-            left = pltpu.roll(other, LANES - LEFT_AT - 4, axis=2) * flag_left
-            right = pltpu.roll(other, LANES - RIGHT_AT - 8, axis=2) * flag_right
-            own = own + jnp.where(lane3 < 8, left, 0.0) + jnp.where(lane3 >= LANES - 8, right, 0.0)
-            sums.append(own)
-            if d == 1:
-                after = other + pltpu.roll(other, LANES - RIGHT_AT - 8, axis=2)
-        if len(along) == 3:
-            sums.append(after)
-            along = [*along, 1]
+    def coarse(sums, along):
         count = len(along)
         stack = jnp.concatenate(sums, axis=0).reshape(2 * count * NZ, LANES)
         blocks = jnp.dot(stack, pick, precision=lax.Precision.HIGHEST, preferred_element_type=F32)
@@ -379,14 +396,15 @@
                 perm[at][n] = both[0] / (both[1] + EPS * extents[d] * extents[d])
         return perm
 
-    perm = coarse(0, range(3), (i < n_gx - 1).astype(F32), (i > 0).astype(F32))
+    sums = [columns(lower_sums(d, 0, e_at(1, last, d, 3), flag_up, flag_low) + upper_sums(d)) for d in range(3)]
+    perm = coarse([own for own, _ in sums] + [sums[1][1]], (0, 1, 2, 1))
     mess[pl.ds(0, NCL)] = jnp.concatenate(perm[0], axis=0)
 
     tell_k = len(copies)
     tell = remote(tell_k, mess, mess_x, -1, 0)
-    sends = inside(-1, 0) & jnp.logical_not(reaches(-1))
+    sends = odd
     pl.when(sends)(tell.start)
-    copies.append((tell, sends, inside(1, 0)))
+    copies.append((tell, sends, even & inside(1, 0)))
     for d in range(3):
         for n in range(NCL):
             perm_ref[d, n] = perm[d][n][:, 0 : LANES // BXY]
@@ -401,26 +419,21 @@
         after = jnp.where(lane1 == LANES // BXY - 1, beyond, pltpu.roll(perm[1][n], LANES - 1, axis=1))
         trans_ref[1, n] = harmonic(perm[1][n], after)[:, 0 : LANES // BXY]
 
-    @pl.when(reaches(0))
+    @pl.when(odd)
     def _():
-        for k in range(8, 13):
-            arrive(k)
-        for c, r in PLANES[len(DOWN) :]:
-            assemble(c, r + 8)
-        for c, r in DOWN:
-            assemble(c, r + 16)
-        for r in [8] + list(range(12, 20)):
-            coefficients(r)
+        arrive(tell_k - 1)
         for s in range(1, SWEEPS):
-            for r in range(12 - s, 20 - s):
+            for r in range(12 - s, 12):
                 main_row(s, r, (0,))
-            for e in (2, 3):
-                for n in range(s + 1):
-                    edge_row(e, s, n, (0,))
-        (beyond,) = coarse(8, (0,), (i + 2 < n_gx).astype(F32), 1.0)
-        mess_x[pl.ds(0, NCL)] = jnp.concatenate(beyond, axis=0)
-
-    @pl.when(jnp.logical_not(reaches(0)))
+            for n in range(s + 1):
+                edge_row(2, s, n, (0,))
+        ended = jnp.concatenate([heard[pl.ds(SWEEPS, 1)], heard[pl.ds(2 * SWEEPS + 1, 1)]], axis=2)
+        own, _ = columns(lower_sums(0, 8, ended, (i + 2 < n_gx).astype(F32), 1.0))
+        (beyond,) = coarse([own + heard[pl.ds(2 * SWEEPS + 2, 2)]], (0,))
+        here = (i + 1 < n_gx).astype(F32)
+        mess_x[pl.ds(0, NCL)] = jnp.concatenate(beyond, axis=0) * here
+
+    @pl.when(even)
     def _():
         arrive(tell_k)
 
@@ -449,29 +462,29 @@
                 vmem(len(PLANES), NZ, LANES),
                 vmem(NZ, LANES),
                 vmem(4, NZ, LANES),
+                vmem(2, NZ, LANES),
                 vmem(len(UP), NZ, LANES),
                 vmem(len(DOWN), NZ, LANES),
-                vmem(len(PLANES) - len(DOWN), NZ, LANES),
-                vmem(len(DOWN), NZ, LANES),
+                vmem(3, NZ, LANES),
                 vmem(4, NZ, LANES),
-                vmem(4, NZ, LANES),
-                vmem(2, NZ, LANES),
-                vmem(4, NZ, LANES),
-                vmem(2, NZ, LANES),
-                vmem(3, 25, NZ, both),
-                vmem(9, 23, NZ, both),
-                vmem(3, 16, NZ, both),
-                vmem(3, 23, NZ, both),
-                vmem(3, 21, NZ, both),
-                vmem(3, 19, NZ, both),
+                vmem(NZ, LANES),
+                vmem(NZ, LANES),
+                vmem(2 * SWEEPS + 4, NZ, LANES),
+                vmem(2 * SWEEPS + 4, NZ, LANES),
                 vmem(3, 17, NZ, both),
-                vmem(4, 9, NZ, both),
-                vmem(4, SWEEPS, 3, SWEEPS, NZ, both),
+                vmem(9, 15, NZ, both),
+                vmem(3, 12, NZ, both),
+                vmem(3, 15, NZ, both),
+                vmem(3, 14, NZ, both),
+                vmem(3, 13, NZ, both),
+                vmem(3, 12, NZ, both),
+                vmem(3, 9, NZ, both),
+                vmem(3, SWEEPS, 3, SWEEPS, NZ, both),
                 vmem(NZ, LANES),
                 vmem(NZ, LANES),
                 pltpu.SemaphoreType.DMA((2,)),
-                pltpu.SemaphoreType.DMA((14,)),
-                pltpu.SemaphoreType.DMA((14,)),
+                pltpu.SemaphoreType.DMA((10,)),
+                pltpu.SemaphoreType.DMA((10,)),
             ],
             compiler_params=pltpu.CompilerParams(
                 collective_id=0, has_side_effects=True, vmem_limit_bytes=32 * 1024 * 1024

time: 31.5 us -> 29.5 us (0.937)
  the two profiles are of different devices: /device:TPU:41 before, /device:TPU:23 now
where the time goes in v5:
time: 29.5 us; the launch traced here: 29.4 us
  Pallas kernels  27.6 us (94%)
  local copies, waits for them, and re-layouts  1.19 us (4%)
  between operations  0.64 us (2%)
    pallas_call x1, Pallas kernels, local(): pl.pallas_call(lambda *refs: kernel(n_gx, n_gy, *refs), out_shape=(out, o...  27.6 us
    unnamed x2, local copies, waits for them, and re-layouts  1.19 us

profile of v5, /device:TPU:23, one launch (start us, length us, event | category | flops | bytes accessed | tf_op | source)
XLA Modules:
  0.0 29.4 jit_solution(4346067379554374163)
XLA Ops:
  0.6 27.6 %upscale.1 = (f32[3,4,1,16]{3,2,1,0:T(1,128)S(1)}, f32[3,4,1,16]{3,2,1,0:T(1,128)S(1)}) custom-call(f32[192,128]{1,0:T(8,128)} %bitcast.1, s32[8]{0:T(128)} %refs_1_.1), custom_call_target="tpu_custom_call" | custom-call | tf_op jit(solution)/shard_map/upscale/pallas_call | solution.py:454
  28.2 0.6 %copy.6 = f32[3,4,1,16]{3,2,1,0:T(1,128)} copy(f32[3,4,1,16]{3,2,1,0:T(1,128)S(1)} %get-tuple-element.4) | data formatting | bytes 1536
  28.8 0.6 %copy.7 = f32[3,4,1,16]{3,2,1,0:T(1,128)} copy(f32[3,4,1,16]{3,2,1,0:T(1,128)S(1)} %get-tuple-element.5) | data formatting | bytes 1536

commit v6 on v5

--- a/solution.py
+++ b/solution.py
@@ -143,7 +143,8 @@
         return remote(k, corners.at[0], high_pack, di, dj)
 
     copies = [(copy_of(k, *to), inside(*to), inside(-to[0], -to[1])) for k, to in enumerate(DIRECTIONS)]
-    for copy, sends, _ in copies:
+    for k in (7, 6, 5, 4, 3, 2, 1, 0):
+        copy, sends, _ = copies[k]
         pl.when(sends)(copy.start)
 
     def arrive(k):
@@ -344,12 +345,12 @@
         for r in range(7, 12):
             coefficients(r)
 
-    def sweeps(starts, stops, e):
+    def sweeps(starts, stops, e, along=range(3)):
         for s in range(1, SWEEPS):
             for r in range(starts[s - 1], stops[s - 1]):
-                main_row(s, r, range(3) if r < 12 - s - 1 else (0,))
+                main_row(s, r, [d for d in along if d == 0 or r < 12 - s - 1])
             for n in range(s + 1):
-                edge_row(e, s, n)
+                edge_row(e, s, n, along)
 
     told = remote(len(copies), tale, heard, -1, 0)
     tells = even & (i > 0)
@@ -358,13 +359,14 @@
     @pl.when(even)
     def _():
         from_above()
-        sweeps((2, 3, 4), (11, 10, 9), 1)
+        sweeps((2, 3, 4), (11, 10, 9), 1, (0,))
         for s in range(SWEEPS + 1):
             value = q_at(s, 0, 4) if s < SWEEPS else e_at(1, last, 0, 3)
             tale[pl.ds(s, 1)] = value[:, :, 0:LANES]
             tale[pl.ds(SWEEPS + 1 + s, 1)] = value[:, :, LANES : 2 * LANES]
         tale[pl.ds(2 * SWEEPS + 2, 2)] = columns(upper_sums(0))[0]
         pl.when(tells)(told.start)
+        sweeps((2, 3, 4), (11, 10, 9), 1, (1, 2))
         from_below()
         sweeps((-2, -1, 0), (2, 3, 4), 0)
 

time: 29.5 us -> 27.8 us (0.942)
  the two profiles are of different devices: /device:TPU:23 before, /device:TPU:31 now
where the time goes in v6:
time: 27.8 us; the launch traced here: 27.7 us
  Pallas kernels  25.8 us (93%)
  local copies, waits for them, and re-layouts  1.19 us (4%)
  between operations  0.64 us (2%)
    pallas_call x1, Pallas kernels, local(): pl.pallas_call(lambda *refs: kernel(n_gx, n_gy, *refs), out_shape=(out, o...  25.8 us
    unnamed x2, local copies, waits for them, and re-layouts  1.19 us

profile of v6, /device:TPU:31, one launch (start us, length us, event | category | flops | bytes accessed | tf_op | source)
XLA Modules:
  0.0 27.7 jit_solution(1070564896647461317)
XLA Ops:
  0.6 25.8 %upscale.1 = (f32[3,4,1,16]{3,2,1,0:T(1,128)S(1)}, f32[3,4,1,16]{3,2,1,0:T(1,128)S(1)}) custom-call(f32[192,128]{1,0:T(8,128)} %bitcast.1, s32[8]{0:T(128)} %refs_1_.1), custom_call_target="tpu_custom_call" | custom-call | tf_op jit(solution)/shard_map/upscale/pallas_call | solution.py:456
  26.5 0.6 %copy.6 = f32[3,4,1,16]{3,2,1,0:T(1,128)} copy(f32[3,4,1,16]{3,2,1,0:T(1,128)S(1)} %get-tuple-element.4) | data formatting | bytes 1536
  27.1 0.6 %copy.7 = f32[3,4,1,16]{3,2,1,0:T(1,128)} copy(f32[3,4,1,16]{3,2,1,0:T(1,128)S(1)} %get-tuple-element.5) | data formatting | bytes 1536

commit v7 on v6

--- a/solution.py
+++ b/solution.py
@@ -62,13 +62,14 @@
 
 
 def kernel(
-    n_gx, n_gy, k_hbm, map_hbm, perm_ref, trans_ref,
+    n_gx, n_gy, k_hbm, map_hbm, out_ref,
     k_own, map_own, planes, lasts, packs, corners, from_low, from_high,
     near_lasts, own_packs, low_pack, high_pack, tale, heard,
     kp, coef, face, q1, q2, q3, q4, u_coef, uq, mess, mess_x,
     load_sem, send_sem, recv_sem,
 ):
     i, j = lax.axis_index("gx"), lax.axis_index("gy")
+    perm_ref, trans_ref = out_ref.at[0], out_ref.at[1]
     load_k = pltpu.make_async_copy(k_hbm, k_own, load_sem.at[0])
     load_map = pltpu.make_async_copy(map_hbm, map_own, load_sem.at[1])
     load_k.start()
@@ -450,14 +451,14 @@
 
     def local(permeability, layer_map):
         k = permeability.reshape(3 * NZ * BXY, LANES)
-        out = jax.ShapeDtypeStruct((3, NCL, 1, LANES // BXY), F32)
+        out = jax.ShapeDtypeStruct((2, 3, NCL, 1, LANES // BXY), F32)
         vmem = lambda *shape: pltpu.VMEM(shape, F32)
         both = 2 * LANES
-        return pl.pallas_call(
+        both_out = pl.pallas_call(
             lambda *refs: kernel(n_gx, n_gy, *refs),
-            out_shape=(out, out),
+            out_shape=out,
             in_specs=[pl.BlockSpec(memory_space=pltpu.HBM)] * 2,
-            out_specs=(pl.BlockSpec(memory_space=pltpu.VMEM),) * 2,
+            out_specs=pl.BlockSpec(memory_space=pltpu.VMEM),
             scratch_shapes=[
                 vmem(3 * NZ * BXY, LANES),
                 pltpu.SMEM((NZ,), jnp.int32),
@@ -493,6 +494,7 @@
             ),
             name="upscale",
         )(pltpu.with_memory_space_constraint(k, pltpu.HBM), pltpu.with_memory_space_constraint(layer_map, pltpu.HBM))
+        return both_out[0], both_out[1]
 
     spec = P(None, None, "gx", "gy")
     return jax.shard_map(local, mesh=mesh, in_specs=(spec, P()), out_specs=(spec, spec), check_vma=False)

time: 27.8 us -> 27.2 us (0.978)
  local copies, waits for them, and re-layouts: 1.19 us -> 0.6 us
    unnamed x2 -> x1, local copies, waits for them, and re-layouts: 1.19 us -> 0.6 us
where the time goes in v7:
time: 27.2 us; the launch traced here: 27.1 us
  Pallas kernels  25.8 us (95%)
  between operations  0.64 us (2%)
  local copies, waits for them, and re-layouts  0.6 us (2%)
    pallas_call x1, Pallas kernels, local(): pl.pallas_call(lambda *refs: kernel(n_gx, n_gy, *refs), out_shape=out, in...  25.8 us
    unnamed x1, local copies, waits for them, and re-layouts  0.6 us

profile of v7, /device:TPU:31, one launch (start us, length us, event | category | flops | bytes accessed | tf_op | source)
XLA Modules:
  0.0 27.1 jit_solution(14923069963897848700)
XLA Ops:
  0.6 25.8 %upscale.1 = f32[2,3,4,1,16]{4,3,2,1,0:T(1,128)S(1)} custom-call(f32[192,128]{1,0:T(8,128)} %bitcast.9, s32[8]{0:T(128)} %refs_1_.1), custom_call_target="tpu_custom_call" | custom-call | tf_op jit(solution)/shard_map/upscale/pallas_call | solution.py:457
  26.5 0.6 %slice_bitcast_fusion = (f32[3,4,1,16]{3,2,1,0:T(1,128)}, f32[3,4,1,16]{3,2,1,0:T(1,128)}) fusion(f32[2,3,4,1,16]{4,3,2,1,0:T(1,128)S(1)} %upscale.1), kind=kLoop, calls=%fused_computation | loop fusion | bytes 3072

commit v8 on v7

--- a/solution.py
+++ b/solution.py
@@ -44,8 +44,11 @@
 DIRECTIONS = [(1, 0), (-1, 0), (1, 1), (1, -1), (-1, 1), (-1, -1), (0, 1), (0, -1)]
 LOW, HIGH, OWN = range(3)
 ENDS = [0, 7, 8]
-LEFT_AT = 20
-RIGHT_AT = 72
+LEFT_AT = 13
+RIGHT_AT = 25
+TOLD = SWEEPS + 1
+SPAN = 42
+TALE = TOLD + -(-TOLD // 3) + 2
 W = [1.0 / (1.05 + 0.95 * math.cos(math.pi * (2 * s + 1) / (2 * SWEEPS))) for s in range(SWEEPS)]
 
 
@@ -252,9 +255,13 @@
 
     qs = [(q1, 3), (q2, 2), (q3, 1), (q4, 0)]
 
+    def told_row(n):
+        other = pltpu.roll(heard[pl.ds(TOLD + n // 3, 1)], LANES - 2 - SPAN * (n % 3), axis=2)
+        return jnp.concatenate([heard[pl.ds(n, 1)], other], axis=2)
+
     def q_at(s, d, r):
         if r == 12:
-            return jnp.concatenate([heard[pl.ds(s, 1)], heard[pl.ds(SWEEPS + 1 + s, 1)]], axis=2)
+            return told_row(s)
         ref, offset = qs[s]
         return ref[d, pl.ds(r + offset, 1)]
 
@@ -361,11 +368,16 @@
     def _():
         from_above()
         sweeps((2, 3, 4), (11, 10, 9), 1, (0,))
-        for s in range(SWEEPS + 1):
-            value = q_at(s, 0, 4) if s < SWEEPS else e_at(1, last, 0, 3)
-            tale[pl.ds(s, 1)] = value[:, :, 0:LANES]
-            tale[pl.ds(SWEEPS + 1 + s, 1)] = value[:, :, LANES : 2 * LANES]
-        tale[pl.ds(2 * SWEEPS + 2, 2)] = columns(upper_sums(0))[0]
+        lane3 = lane_of((1, NZ, LANES))
+        others = [None, None]
+        for n in range(TOLD):
+            value = q_at(n, 0, 4) if n < SWEEPS else e_at(1, last, 0, 3)
+            tale[pl.ds(n, 1)] = value[:, :, 0:LANES]
+            other = pltpu.roll(value[:, :, LANES : 2 * LANES], 2 + SPAN * (n % 3), axis=2)
+            others[n // 3] = other if n % 3 == 0 else jnp.where(lane3 >= SPAN * (n % 3), other, others[n // 3])
+        for n, other in enumerate(others):
+            tale[pl.ds(TOLD + n, 1)] = other
+        tale[pl.ds(TALE - 2, 2)] = columns(upper_sums(0))[0]
         pl.when(tells)(told.start)
         sweeps((2, 3, 4), (11, 10, 9), 1, (1, 2))
         from_below()
@@ -430,9 +442,9 @@
                 main_row(s, r, (0,))
             for n in range(s + 1):
                 edge_row(2, s, n, (0,))
-        ended = jnp.concatenate([heard[pl.ds(SWEEPS, 1)], heard[pl.ds(2 * SWEEPS + 1, 1)]], axis=2)
+        ended = told_row(SWEEPS)
         own, _ = columns(lower_sums(0, 8, ended, (i + 2 < n_gx).astype(F32), 1.0))
-        (beyond,) = coarse([own + heard[pl.ds(2 * SWEEPS + 2, 2)]], (0,))
+        (beyond,) = coarse([own + heard[pl.ds(TALE - 2, 2)]], (0,))
         here = (i + 1 < n_gx).astype(F32)
         mess_x[pl.ds(0, NCL)] = jnp.concatenate(beyond, axis=0) * here
 
@@ -472,8 +484,8 @@
                 vmem(4, NZ, LANES),
                 vmem(NZ, LANES),
                 vmem(NZ, LANES),
-                vmem(2 * SWEEPS + 4, NZ, LANES),
-                vmem(2 * SWEEPS + 4, NZ, LANES),
+                vmem(TALE, NZ, LANES),
+                vmem(TALE, NZ, LANES),
                 vmem(3, 17, NZ, both),
                 vmem(9, 15, NZ, both),
                 vmem(3, 12, NZ, both),

time: 27.2 us -> 27 us (level)
  no operation moved by 1% of the time
where the time goes in v8:
time: 27 us; the launch traced here: 26.9 us
  Pallas kernels  25.6 us (95%)
  between operations  0.64 us (2%)
  local copies, waits for them, and re-layouts  0.6 us (2%)
    pallas_call x1, Pallas kernels, local(): pl.pallas_call(lambda *refs: kernel(n_gx, n_gy, *refs), out_shape=out, in...  25.6 us
    unnamed x1, local copies, waits for them, and re-layouts  0.6 us

profile of v8, /device:TPU:31, one launch (start us, length us, event | category | flops | bytes accessed | tf_op | source)
XLA Modules:
  0.0 26.9 jit_solution(784510185729753100)
XLA Ops:
  0.6 25.6 %upscale.1 = f32[2,3,4,1,16]{4,3,2,1,0:T(1,128)S(1)} custom-call(f32[192,128]{1,0:T(8,128)} %bitcast.9, s32[8]{0:T(128)} %refs_1_.1), custom_call_target="tpu_custom_call" | custom-call | tf_op jit(solution)/shard_map/upscale/pallas_call | solution.py:469
  26.3 0.6 %slice_bitcast_fusion = (f32[3,4,1,16]{3,2,1,0:T(1,128)}, f32[3,4,1,16]{3,2,1,0:T(1,128)}) fusion(f32[2,3,4,1,16]{4,3,2,1,0:T(1,128)S(1)} %upscale.1), kind=kLoop, calls=%fused_computation | loop fusion | bytes 3072

commit v9 on v8

--- a/solution.py
+++ b/solution.py
@@ -149,7 +149,7 @@
     copies = [(copy_of(k, *to), inside(*to), inside(-to[0], -to[1])) for k, to in enumerate(DIRECTIONS)]
     for k in (7, 6, 5, 4, 3, 2, 1, 0):
         copy, sends, _ = copies[k]
-        pl.when(sends)(copy.start)
+        pl.when(sends & even if k == 0 else sends)(copy.start)
 
     def arrive(k):
         copy, _, here = copies[k]
@@ -336,6 +336,8 @@
             assemble(c, r)
     for r in range(1, 7):
         coefficients(r)
+
+    pl.when(odd & copies[0][1])(copies[0][0].start)
 
     def from_below():
         for k in (2, 3, 0):

time: 27 us -> 26.4 us (0.978)
  Pallas kernels: 25.6 us -> 25 us
    pallas_call x1, Pallas kernels: 25.6 us -> 25 us  [local(): pl.pallas_call(lambda *refs: kernel(n_gx, n_gy, *refs), out_shape=out, in...]
where the time goes in v9:
time: 26.4 us; the launch traced here: 26.2 us
  Pallas kernels  25 us (95%)
  between operations  0.64 us (2%)
  local copies, waits for them, and re-layouts  0.6 us (2%)
    pallas_call x1, Pallas kernels, local(): pl.pallas_call(lambda *refs: kernel(n_gx, n_gy, *refs), out_shape=out, in...  25 us
    unnamed x1, local copies, waits for them, and re-layouts  0.6 us

profile of v9, /device:TPU:31, one launch (start us, length us, event | category | flops | bytes accessed | tf_op | source)
XLA Modules:
  0.0 26.2 jit_solution(14487312893523472276)
XLA Ops:
  0.6 25.0 %upscale.1 = f32[2,3,4,1,16]{4,3,2,1,0:T(1,128)S(1)} custom-call(f32[192,128]{1,0:T(8,128)} %bitcast.9, s32[8]{0:T(128)} %refs_1_.1), custom_call_target="tpu_custom_call" | custom-call | tf_op jit(solution)/shard_map/upscale/pallas_call | solution.py:471
  25.6 0.6 %slice_bitcast_fusion = (f32[3,4,1,16]{3,2,1,0:T(1,128)}, f32[3,4,1,16]{3,2,1,0:T(1,128)}) fusion(f32[2,3,4,1,16]{4,3,2,1,0:T(1,128)S(1)} %upscale.1), kind=kLoop, calls=%fused_computation | loop fusion | bytes 3072

commit v10 on v8

--- a/solution.py
+++ b/solution.py
@@ -149,7 +149,7 @@
     copies = [(copy_of(k, *to), inside(*to), inside(-to[0], -to[1])) for k, to in enumerate(DIRECTIONS)]
     for k in (7, 6, 5, 4, 3, 2, 1, 0):
         copy, sends, _ = copies[k]
-        pl.when(sends)(copy.start)
+        pl.when(sends & even if k in (0, 2, 3) else sends)(copy.start)
 
     def arrive(k):
         copy, _, here = copies[k]
@@ -336,6 +336,9 @@
             assemble(c, r)
     for r in range(1, 7):
         coefficients(r)
+
+    for k in (0, 2, 3):
+        pl.when(odd & copies[k][1])(copies[k][0].start)
 
     def from_below():
         for k in (2, 3, 0):

time: 27 us -> 26.4 us (0.978)
  Pallas kernels: 25.6 us -> 25 us
    pallas_call x1, Pallas kernels: 25.6 us -> 25 us  [local(): pl.pallas_call(lambda *refs: kernel(n_gx, n_gy, *refs), out_shape=out, in...]
where the time goes in v10:
time: 26.4 us; the launch traced here: 26.2 us
  Pallas kernels  25 us (95%)
  between operations  0.64 us (2%)
  local copies, waits for them, and re-layouts  0.6 us (2%)
    pallas_call x1, Pallas kernels, local(): pl.pallas_call(lambda *refs: kernel(n_gx, n_gy, *refs), out_shape=out, in...  25 us
    unnamed x1, local copies, waits for them, and re-layouts  0.6 us

profile of v10, /device:TPU:31, one launch (start us, length us, event | category | flops | bytes accessed | tf_op | source)
XLA Modules:
  0.0 26.2 jit_solution(13413268832760076247)
XLA Ops:
  0.6 25.0 %upscale.1 = f32[2,3,4,1,16]{4,3,2,1,0:T(1,128)S(1)} custom-call(f32[192,128]{1,0:T(8,128)} %bitcast.9, s32[8]{0:T(128)} %refs_1_.1), custom_call_target="tpu_custom_call" | custom-call | tf_op jit(solution)/shard_map/upscale/pallas_call | solution.py:472
  25.6 0.6 %slice_bitcast_fusion = (f32[3,4,1,16]{3,2,1,0:T(1,128)}, f32[3,4,1,16]{3,2,1,0:T(1,128)}) fusion(f32[2,3,4,1,16]{4,3,2,1,0:T(1,128)S(1)} %upscale.1), kind=kLoop, calls=%fused_computation | loop fusion | bytes 3072
